TPU v7x, 512 devices: a whole 4x8x8 slice. The times are simulated.
512 devices in a mesh: gx: 32 (over z, y_lo, core), gy: 16 (over x, y_hi).
Axes of the slice: x: 4, y: 8 (y_hi: 4, y_lo: 2; y = y_hi * 2 + y_lo), z: 8, core: 2. Of those that a mesh axis runs over, the one named last changes fastest.
Arguments:
- potential: float32 [128, 256, 256], P('gx', 'gy'), may hold values from -0.2 to 1.2
- recovery: float32 [128, 256, 256], P('gx', 'gy'), may hold values from 0 to 1.5
- fiber_angles: float32 [2, 128, 256, 256], P(None, 'gx', 'gy'), may hold values from -3.140625 to 3.140625
- deform: float32 [9, 131072], P(None, ('gx', 'gy')), may hold values from -0.15 to 1.25, as said below
- elem_slot: int32 [32, 64, 64], P('gx', 'gy'), may hold values from 0 to 131071, as said below
Outputs:
- potential_next: float32 [128, 256, 256], P('gx', 'gy')
- recovery_next: float32 [128, 256, 256], P('gx', 'gy')
Inputs may be any that keep to these rules, and one draw needn't show every extreme that they name: `elem_slot`: entries are distinct. Slot s lies on device s / 256 (rounded down) of gx+gy. The elements of one device's block along gx and gy lie in the slots of the devices with the same index along gx, exactly 16 of them in each. `deform`: components 0, 4 and 8 (the diagonal of F) lie in 0.8 to 1.25, the other six in -0.15 to 0.15.
All inputs are finite; a program needn't handle non-finite values.
Results may differ from a plain program's by a relative error of at most 0.0003.
Values sent between devices are 32-bit elements; how exact they have to be, the bound alone decides.
A program may use at most 64 MiB of HBM per device.

v0:
```python
import jax
import jax.numpy as jnp
from jax import lax
from jax.sharding import PartitionSpec as P

RATIO = 4


sigma_fiber = 1.0
sigma_cross = 0.3
time_step = 0.1
excite_gain = 8.0
excite_level = 0.15
stretch_gain = 10.0
stretch_reversal = 0.6
recover_rate = 0.5


def padded_2(block, sides, width):
    for axis, dim in sides:
        count = lax.axis_size(axis)
        forward = [(i, i + 1) for i in range(count - 1)]
        backward = [(target, source) for source, target in forward]
        low = lax.ppermute(
            lax.slice_in_dim(block, block.shape[dim] - width, None, axis=dim), axis, forward
        )
        high = lax.ppermute(lax.slice_in_dim(block, 0, width, axis=dim), axis, backward)
        block = jnp.concatenate([low, block, high], axis=dim)
    return block


def refine(padded, dim):
    inner_size = padded.shape[dim] - 2
    lower = lax.slice_in_dim(padded, 0, inner_size, axis=dim)
    middle = lax.slice_in_dim(padded, 1, inner_size + 1, axis=dim)
    upper = lax.slice_in_dim(padded, 2, inner_size + 2, axis=dim)
    pieces = []
    for position in range(RATIO):
        offset = (position + 0.5) / RATIO - 0.5
        weight = abs(offset)
        neighbor = lower if offset < 0 else upper
        pieces.append((1.0 - weight) * middle + weight * neighbor)
    stacked = jnp.stack(pieces, axis=dim + 1)
    new_shape = list(padded.shape)
    new_shape[dim] = inner_size * RATIO
    return stacked.reshape(new_shape)


def refine_wide(padded, dim):
    weight = 0.5 - 0.5 / RATIO
    extent = padded.shape[dim]
    low_rim = (1.0 - weight) * lax.slice_in_dim(padded, 0, 1, axis=dim) + weight * lax.slice_in_dim(
        padded, 1, 2, axis=dim
    )
    high_rim = (1.0 - weight) * lax.slice_in_dim(
        padded, extent - 1, extent, axis=dim
    ) + weight * lax.slice_in_dim(padded, extent - 2, extent - 1, axis=dim)
    return jnp.concatenate([low_rim, refine(padded, dim), high_rim], axis=dim)


def directions(angles):
    azimuth = angles[0]
    elevation = angles[1]
    return jnp.stack(
        [
            jnp.cos(azimuth) * jnp.cos(elevation),
            jnp.sin(azimuth) * jnp.cos(elevation),
            jnp.sin(elevation),
        ]
    )


def tensors(field, fiber):
    entries = [field[number] for number in range(9)]

    def element(row_index, col_index):
        return entries[3 * (row_index % 3) + col_index % 3]

    cofactor = [
        [
            element(row_index + 1, col_index + 1) * element(row_index + 2, col_index + 2)
            - element(row_index + 1, col_index + 2) * element(row_index + 2, col_index + 1)
            for col_index in range(3)
        ]
        for row_index in range(3)
    ]
    determinant = (
        element(0, 0) * cofactor[0][0]
        + element(0, 1) * cofactor[0][1]
        + element(0, 2) * cofactor[0][2]
    )
    inverse = [
        [cofactor[col_index][row_index] / determinant for col_index in range(3)]
        for row_index in range(3)
    ]
    stretched = [
        element(row_index, 0) * fiber[0]
        + element(row_index, 1) * fiber[1]
        + element(row_index, 2) * fiber[2]
        for row_index in range(3)
    ]
    stretch = jnp.sqrt(
        stretched[0] * stretched[0] + stretched[1] * stretched[1] + stretched[2] * stretched[2]
    )
    pulled = [
        inverse[row_index][0] * fiber[0]
        + inverse[row_index][1] * fiber[1]
        + inverse[row_index][2] * fiber[2]
        for row_index in range(3)
    ]
    conduct = []
    for first_index, second_index in ((0, 0), (1, 1), (2, 2), (0, 1), (0, 2), (1, 2)):
        metric = (
            inverse[first_index][0] * inverse[second_index][0]
            + inverse[first_index][1] * inverse[second_index][1]
            + inverse[first_index][2] * inverse[second_index][2]
        )
        conduct.append(
            sigma_cross * metric
            + (sigma_fiber - sigma_cross) * pulled[first_index] * pulled[second_index]
        )
    return (jnp.stack(conduct), stretch)


def close_faces(flux, dim, at_first, at_last):
    extent = flux.shape[dim]
    face_index = lax.broadcasted_iota(jnp.int32, flux.shape, dim)
    closed = (face_index == 0) & at_first | (face_index == extent - 1) & at_last
    return jnp.where(closed, jnp.zeros_like(flux), flux)


def divergence(potential_pad, tensor_pad, first_x, last_x, first_y, last_y):
    grad_x = (potential_pad[2:, :, :] - potential_pad[:-2, :, :]) * 0.5
    grad_y = (potential_pad[:, 2:, :] - potential_pad[:, :-2, :]) * 0.5
    grad_z = (potential_pad[:, :, 2:] - potential_pad[:, :, :-2]) * 0.5

    def face_mean(component, dim):
        inner = tensor_pad[component]
        if dim == 0:
            inner = inner[:, 1:-1, 1:-1]
        elif dim == 1:
            inner = inner[1:-1, :, 1:-1]
        else:
            inner = inner[1:-1, 1:-1, :]
        extent = inner.shape[dim]
        return (
            lax.slice_in_dim(inner, 1, extent, axis=dim)
            + lax.slice_in_dim(inner, 0, extent - 1, axis=dim)
        ) * 0.5

    step_x = potential_pad[1:, 1:-1, 1:-1] - potential_pad[:-1, 1:-1, 1:-1]
    mean_y = (grad_y[1:, :, 1:-1] + grad_y[:-1, :, 1:-1]) * 0.5
    mean_z = (grad_z[1:, 1:-1, :] + grad_z[:-1, 1:-1, :]) * 0.5
    flux_x = face_mean(0, 0) * step_x + face_mean(3, 0) * mean_y + face_mean(4, 0) * mean_z
    flux_x = close_faces(flux_x, 0, first_x, last_x)
    step_y = potential_pad[1:-1, 1:, 1:-1] - potential_pad[1:-1, :-1, 1:-1]
    mean_x = (grad_x[:, 1:, 1:-1] + grad_x[:, :-1, 1:-1]) * 0.5
    mean_z = (grad_z[1:-1, 1:, :] + grad_z[1:-1, :-1, :]) * 0.5
    flux_y = face_mean(3, 1) * mean_x + face_mean(1, 1) * step_y + face_mean(5, 1) * mean_z
    flux_y = close_faces(flux_y, 1, first_y, last_y)
    step_z = potential_pad[1:-1, 1:-1, 1:] - potential_pad[1:-1, 1:-1, :-1]
    mean_x = (grad_x[:, 1:-1, 1:] + grad_x[:, 1:-1, :-1]) * 0.5
    mean_y = (grad_y[1:-1, :, 1:] + grad_y[1:-1, :, :-1]) * 0.5
    flux_z = face_mean(4, 2) * mean_x + face_mean(5, 2) * mean_y + face_mean(2, 2) * step_z
    flux_z = close_faces(flux_z, 2, True, True)
    return (
        flux_x[1:]
        - flux_x[:-1]
        + (flux_y[:, 1:] - flux_y[:, :-1])
        + (flux_z[:, :, 1:] - flux_z[:, :, :-1])
    )


def update(voltage, recovery, divergent, stretch):
    current = (
        excite_gain * voltage * (voltage - excite_level) * (voltage - 1.0) + voltage * recovery
    )
    current = current + stretch_gain * jnp.maximum(stretch - 1.0, 0.0) * (
        voltage - stretch_reversal
    )
    voltage_next = voltage + time_step * (divergent - current)
    recovery_next = recovery + time_step * recover_rate * (
        -recovery - excite_gain * voltage * (voltage - excite_level - 1.0)
    )
    return (voltage_next, recovery_next)


def clamp_rim(extended, dim, at_first, at_last):
    extent = extended.shape[dim]
    low_rim = jnp.where(
        at_first,
        lax.slice_in_dim(extended, 1, 2, axis=dim),
        lax.slice_in_dim(extended, 0, 1, axis=dim),
    )
    high_rim = jnp.where(
        at_last,
        lax.slice_in_dim(extended, extent - 2, extent - 1, axis=dim),
        lax.slice_in_dim(extended, extent - 1, extent, axis=dim),
    )
    return jnp.concatenate(
        [low_rim, lax.slice_in_dim(extended, 1, extent - 1, axis=dim), high_rim], axis=dim
    )


def pad_last(values):
    widths = [(0, 0)] * (values.ndim - 1) + [(1, 1)]
    return jnp.pad(values, widths, mode="edge")


def local(potential, recovery, fiber_angles, deform, elem_slot):
    block_x, block_y, block_z = elem_slot.shape
    components = deform.shape[0]
    held_count = deform.shape[1]
    across = lax.axis_size("gx")
    down_count = lax.axis_size("gy")
    at_first_x = lax.axis_index("gx") == 0
    at_last_x = lax.axis_index("gx") == across - 1
    at_first_y = lax.axis_index("gy") == 0
    at_last_y = lax.axis_index("gy") == down_count - 1
    flat_slots = elem_slot.reshape(-1)
    sort_order = jnp.argsort(flat_slots)
    wanted = (flat_slots[sort_order] % held_count).reshape(down_count, -1)
    asked_slots = lax.all_to_all(wanted, "gy", split_axis=0, concat_axis=0, tiled=True)
    picked = deform[:, asked_slots.reshape(-1)].reshape(components, down_count, -1)
    answered = lax.all_to_all(picked, "gy", split_axis=1, concat_axis=1, tiled=True)
    coarse = jnp.zeros((components, flat_slots.shape[0]), jnp.float32)
    coarse = coarse.at[:, sort_order].set(answered.reshape(components, -1))
    coarse = coarse.reshape(components, block_x, block_y, block_z)
    coarse = padded_2(coarse, (("gx", 1), ("gy", 2)), 1)
    coarse = pad_last(
        clamp_rim(clamp_rim(coarse, 1, at_first_x, at_last_x), 2, at_first_y, at_last_y)
    )
    fine_field = refine(refine_wide(refine_wide(coarse, 1), 2), 3)
    angles_wide = padded_2(fiber_angles, (("gx", 1), ("gy", 2)), 1)
    conduct, stretch = tensors(fine_field, directions(angles_wide))
    stretch = stretch[1:-1, 1:-1]
    tensor_pad = pad_last(conduct)
    neighbors = padded_2(potential, (("gx", 0), ("gy", 1)), 1)
    potential_pad = pad_last(
        clamp_rim(clamp_rim(neighbors, 0, at_first_x, at_last_x), 1, at_first_y, at_last_y)
    )
    divergent = divergence(potential_pad, tensor_pad, at_first_x, at_last_x, at_first_y, at_last_y)
    return update(potential, recovery, divergent, stretch)


def solution(mesh):
    placed = (
        P("gx", "gy", None),
        P("gx", "gy", None),
        P(None, "gx", "gy", None),
        P(None, ("gx", "gy")),
        P("gx", "gy", None),
    )
    return jax.shard_map(
        local,
        mesh=mesh,
        in_specs=placed,
        out_specs=(P("gx", "gy", None), P("gx", "gy", None)),
        check_vma=False,
    )
```

profile of v0, /device:TPU:262, one launch (start us, length us, event | category | flops | bytes accessed | tf_op | source)
XLA Modules:
  0.0 117.4 jit_solution(9200574766309781175)
XLA Ops:
  0.6 0.8 reshape.1500
  1.4 3.2 %sort.17 = (s32[256]{0:T(256)}, s32[256]{0:T(256)S(1)}) sort(s32[256]{0:T(256)S(1)} %reshape.1500, s32[256]{0:T(256)S(1)} %iota.29), dimensions={0}, to_apply=%region_0.0 | sort | flops 2048 | bytes 4096 | tf_op jit(solution)/shard_map/jit(argsort)/sort | solution.py:221
  4.6 1.9 %gather_fusion = s32[256]{0:T(256)S(1)} fusion(s32[256]{0:T(256)S(1)} %reshape.1500, s32[1024]{0:T(1024)S(1)} %pad_clamp_fusion.1), kind=kCustom, calls=%fused_computation | custom fusion | bytes 3072 | tf_op jit(solution)/shard_map/gather | solution.py:222
  6.6 0.6 and_select_fusion
  7.2 10.1 %all-to-all-start = ((s32[16,1,16]{2,1,0:T(1,128)}), s32[16,1,16]{2,1,0:T(1,128)S(1)}, u32[]{:S(2)}, u32[]{:S(2)}) async-start(s32[16,1,16]{2,1,0:T(1,128)} %and_select_fusion), calls=%async_computation | async-start | bytes 16384 | tf_op jit(solution)/shard_map/all_to_all | solution.py:223
  17.3 0.7 fusion.88
  18.0 1.9 %collective-permute-start.9 = (f32[1,16,256]{2,1,0:T(8,128)S(1)}, f32[1,16,256]{2,1,0:T(8,128)S(1)}, u32[]{:S(2)}, u32[]{:S(2)}) collective-permute-start(f32[1,16,256]{2,1,0:T(8,128)S(1)} %get-tuple-element.87), channel_id=1, source_target_pairs={{16,0},{32,16},{48,32},{64,48},{80,64},{96,80},{112,96},{128,112},... | collective-permute-start | bytes 49160 | tf_op jit(solution)/shard_map/ppermute | solution.py:27
  20.0 2.4 %collective-permute-start.8 = (f32[1,16,256]{2,1,0:T(8,128)S(1)}, f32[1,16,256]{2,1,0:T(8,128)S(1)}, u32[]{:S(2)}, u32[]{:S(2)}) collective-permute-start(f32[1,16,256]{2,1,0:T(8,128)S(1)} %get-tuple-element.88), channel_id=1, source_target_pairs={{0,16},{16,32},{32,48},{48,64},{64,80},{80,96},{96,112},{112,128},... | collective-permute-start | bytes 49160 | tf_op jit(solution)/shard_map/ppermute | solution.py:24
  22.4 0.8 fusion.85
  23.2 5.3 %collective-permute-start.5 = (f32[2,1,16,256]{3,2,1,0:T(8,128)S(1)}, f32[2,1,16,256]{3,2,1,0:T(8,128)S(1)}, u32[]{:S(2)}, u32[]{:S(2)}) collective-permute-start(f32[2,1,16,256]{3,2,1,0:T(8,128)S(1)} %get-tuple-element.64), channel_id=1, source_target_pairs={{16,0},{32,16},{48,32},{64,48},{80,64},{96,80},{112,96},{128,112},... | collective-permute-start | bytes 98312 | tf_op jit(solution)/shard_map/ppermute | solution.py:27
  28.4 1.9 %collective-permute-start.4 = (f32[2,1,16,256]{3,2,1,0:T(8,128)S(1)}, f32[2,1,16,256]{3,2,1,0:T(8,128)S(1)}, u32[]{:S(2)}, u32[]{:S(2)}) collective-permute-start(f32[2,1,16,256]{3,2,1,0:T(8,128)S(1)} %get-tuple-element.65), channel_id=1, source_target_pairs={{0,16},{16,32},{32,48},{48,64},{64,80},{80,96},{96,112},{112,128},... | collective-permute-start | bytes 98312 | tf_op jit(solution)/shard_map/ppermute | solution.py:24
  31.5 0.8 copy.231
  32.8 0.7 reduce.3
  33.6 0.7 gather_fusion.1
  34.3 0.8 reshape.1544
  35.1 9.6 %all-to-all-start.1 = ((f32[16,1,144]{2,1,0:T(1,128)}), f32[16,1,144]{2,1,0:T(1,128)S(1)}, u32[]{:S(2)}, u32[]{:S(2)}) async-start(f32[16,1,144]{2,1,0:T(1,128)} %reshape.1544), calls=%async_computation.1 | async-start | bytes 32768 | tf_op jit(solution)/shard_map/all_to_all | solution.py:225
  44.7 1.6 %multiply_add_fusion.4 = (f32[4,16,256]{2,1,0:T(8,128)}, f32[6,16,256]{2,1,0:T(8,128)S(1)}) fusion(f32[4,16,256]{2,1,0:T(8,128)} %param.6, f32[4,16,256]{2,1,0:T(8,128)} %param.5, f32[6,16,256]{2,1,0:T(8,128)S(1)} %constant_dynamic-update-slice_fusion.5), kind=kLoop, calls=%fused_computation.162 | loop fusion | flops 114688 | bytes 262144 | tf_op jit(solution)/shard_map/add | solution.py:182
  46.3 4.3 %collective-permute-start.10 = (f32[6,1,256]{2,1,0:T(1,128)S(1)}, f32[6,1,256]{2,1,0:T(1,128)S(1)}, u32[]{:S(2)}, u32[]{:S(2)}) collective-permute-start(f32[6,1,256]{2,1,0:T(1,128)S(1)} %get-tuple-element.83), channel_id=1, source_target_pairs={{0,1},{1,2},{2,3},{3,4},{4,5},{5,6},{6,7},{7,8},{8,9},{9,10},{10,1... | collective-permute-start | bytes 18440 | tf_op jit(solution)/shard_map/ppermute | solution.py:24
  50.6 4.6 %collective-permute-start.11 = (f32[6,1,256]{2,1,0:T(1,128)S(1)}, f32[6,1,256]{2,1,0:T(1,128)S(1)}, u32[]{:S(2)}, u32[]{:S(2)}) collective-permute-start(f32[6,1,256]{2,1,0:T(1,128)S(1)} %get-tuple-element.84), channel_id=1, source_target_pairs={{1,0},{2,1},{3,2},{4,3},{5,4},{6,5},{7,6},{8,7},{9,8},{10,9},{11,1... | collective-permute-start | bytes 18440 | tf_op jit(solution)/shard_map/ppermute | solution.py:27
  56.3 0.7 reduce.4
  57.1 1.2 %scatter_custom_fusion = f32[9,256]{0,1:T(8,128)S(1)} fusion(s32[256]{0:T(256)S(1)} %compare_select_fusion.3, f32[256,9]{1,0:T(8,128)S(1)} %bitcast.139, f32[]{:T(128)} %constant.31.clone.1), kind=kCustom, calls=%fused_computation.163 | custom fusion | bytes 9220 | tf_op jit(solution)/shard_map/scatter | solution.py:227
  58.4 4.6 %collective-permute-start.1 = (f32[9,1,4,64]{3,2,0,1:T(4,128)S(1)}, f32[9,1,4,64]{3,2,0,1:T(4,128)S(1)}, u32[]{:S(2)}, u32[]{:S(2)}) collective-permute-start(f32[9,1,4,64]{3,2,0,1:T(4,128)S(1)} %copy.232), channel_id=1, source_target_pairs={{16,0},{32,16},{48,32},{64,48},{80,64},{96,80},{112,96},{128,112},... | collective-permute-start | bytes 27656 | tf_op jit(solution)/shard_map/ppermute | solution.py:27
  63.0 1.9 %collective-permute-start = (f32[9,1,4,64]{3,2,0,1:T(4,128)S(1)}, f32[9,1,4,64]{3,2,0,1:T(4,128)S(1)}, u32[]{:S(2)}, u32[]{:S(2)}) collective-permute-start(f32[9,1,4,64]{3,2,0,1:T(4,128)S(1)} %copy.232), channel_id=1, source_target_pairs={{0,16},{16,32},{32,48},{48,64},{64,80},{80,96},{96,112},{112,128},... | collective-permute-start | bytes 27656 | tf_op jit(solution)/shard_map/ppermute | solution.py:24
  65.7 4.4 %collective-permute-done = f32[9,1,4,64]{3,2,0,1:T(4,128)S(1)} collective-permute-done((f32[9,1,4,64]{3,2,0,1:T(4,128)S(1)}, f32[9,1,4,64]{3,2,0,1:T(4,128)S(1)}, u32[]{:S(2)}, u32[]{:S(2)}) %collective-permute-start) | collective-permute-done | bytes 9248 | tf_op jit(solution)/shard_map/ppermute | solution.py:24
  70.2 3.1 %collective-permute-start.2 = (f32[9,3,1,64]{3,2,0,1:T(1,128)S(1)}, f32[9,3,1,64]{3,2,0,1:T(1,128)S(1)}, u32[]{:S(2)}, u32[]{:S(2)}) collective-permute-start(f32[9,3,1,64]{3,2,0,1:T(1,128)S(1)} %get-tuple-element.89), channel_id=1, source_target_pairs={{0,1},{1,2},{2,3},{3,4},{4,5},{5,6},{6,7},{7,8},{8,9},{9,10},{10,1... | collective-permute-start | bytes 20744 | tf_op jit(solution)/shard_map/ppermute | solution.py:24
  73.3 5.8 %collective-permute-start.3 = (f32[9,3,1,64]{3,2,0,1:T(1,128)S(1)}, f32[9,3,1,64]{3,2,0,1:T(1,128)S(1)}, u32[]{:S(2)}, u32[]{:S(2)}) collective-permute-start(f32[9,3,1,64]{3,2,0,1:T(1,128)S(1)} %get-tuple-element.90), channel_id=1, source_target_pairs={{1,0},{2,1},{3,2},{4,3},{5,4},{6,5},{7,6},{8,7},{9,8},{10,9},{11,1... | collective-permute-start | bytes 20744 | tf_op jit(solution)/shard_map/ppermute | solution.py:27
  79.2 0.6 copy.316
  80.4 2.2 %collective-permute-start.7 = (f32[2,6,1,256]{3,0,2,1:T(2,128)}, f32[2,6,1,256]{3,0,2,1:T(2,128)}, u32[]{:S(2)}, u32[]{:S(2)}) collective-permute-start(f32[2,6,1,256]{3,0,2,1:T(2,128)} %copy.317), channel_id=1, source_target_pairs={{1,0},{2,1},{3,2},{4,3},{5,4},{6,5},{7,6},{8,7},{9,8},{10,9},{11,1... | collective-permute-start | bytes 36872 | tf_op jit(solution)/shard_map/ppermute | solution.py:27
  82.7 4.5 %collective-permute-start.6 = (f32[2,6,1,256]{3,0,2,1:T(2,128)}, f32[2,6,1,256]{3,0,2,1:T(2,128)}, u32[]{:S(2)}, u32[]{:S(2)}) collective-permute-start(f32[2,6,1,256]{3,0,2,1:T(2,128)} %copy.316), channel_id=1, source_target_pairs={{0,1},{1,2},{2,3},{3,4},{4,5},{5,6},{6,7},{7,8},{8,9},{9,10},{10,1... | collective-permute-start | bytes 36872 | tf_op jit(solution)/shard_map/ppermute | solution.py:24
  89.1 1.2 fusion.81
  91.3 1.3 %copy.263 = f32[1,6,18,64,4]{2,4,3,1,0:T(4,128)S(1)} copy(f32[1,6,18,64,4]{3,2,1,0,4:T(8,128)} %get-tuple-element.26) | data formatting | bytes 221184 | tf_op jit(solution)/shard_map/slice | solution.py:74
  93.1 0.8 copy.318
  93.9 1.3 %copy.259 = f32[1,6,18,64,4]{2,4,3,1,0:T(4,128)S(1)} copy(f32[1,6,18,64,4]{3,2,1,0,4:T(8,128)} %get-tuple-element.27) | data formatting | bytes 221184 | tf_op jit(solution)/shard_map/slice | solution.py:74
  95.5 0.9 copy.304
  96.4 1.3 %copy.255 = f32[1,6,18,64,4]{2,4,3,1,0:T(4,128)S(1)} copy(f32[1,6,18,64,4]{3,2,1,0,4:T(8,128)} %get-tuple-element.28) | data formatting | bytes 221184 | tf_op jit(solution)/shard_map/slice | solution.py:74
  98.0 0.9 copy.300
  99.5 0.9 copy.298
  101.3 0.8 copy.321
  102.1 1.3 %copy.249 = f32[1,6,18,64,4]{2,4,3,1,0:T(4,128)S(1)} copy(f32[1,6,18,64,4]{3,2,1,0,4:T(8,128)} %get-tuple-element.31) | data formatting | bytes 221184 | tf_op jit(solution)/shard_map/slice | solution.py:74
  103.9 0.8 copy.319
  105.7 1.3 %copy.245 = f32[1,6,18,64,4]{2,4,3,1,0:T(4,128)S(1)} copy(f32[1,6,18,64,4]{3,2,1,0,4:T(8,128)} %get-tuple-element.33) | data formatting | bytes 221184 | tf_op jit(solution)/shard_map/slice | solution.py:74
  107.6 0.7 copy.280
  108.4 0.7 copy.279
  109.1 1.0 pad_maximum_fusion.4
  110.1 1.5 %fusion.1 = (f32[6,6,18,256]{3,2,1,0:T(8,128)S(1)}, f32[1,6,18,256]{3,2,1,0:T(8,128)S(1)}, f32[1,6,18,256]{3,2,1,0:T(8,128)S(1)}, f32[1,6,18,256]{3,2,1,0:T(8,12...) fusion(f32[2,6,18,256]{3,2,1,0:T(8,128)S(1)} %pad_maximum_fusio, ...), kind=kLoop, calls=%fused_computation.31 | loop fusion | flops 1078271 | bytes 2543616
  111.6 0.6 fusion.7
  112.2 0.6 fusion.11
  116.6 0.8 fusion.63
  (124 shorter events, 15.4 us)
Async XLA Ops:
  7.2 25.0 %all-to-all-start = ((s32[16,1,16]{2,1,0:T(1,128)}), s32[16,1,16]{2,1,0:T(1,128)S(1)}, u32[]{:S(2)}, u32[]{:S(2)}) async-start(s32[16,1,16]{2,1,0:T(1,128)} %and_select_fusion), calls=%async_computation | async-start | bytes 16384 | tf_op jit(solution)/shard_map/all_to_all | solution.py:223
  18.0 28.2 %collective-permute-start.9 = (f32[1,16,256]{2,1,0:T(8,128)S(1)}, f32[1,16,256]{2,1,0:T(8,128)S(1)}, u32[]{:S(2)}, u32[]{:S(2)}) collective-permute-start(f32[1,16,256]{2,1,0:T(8,128)S(1)} %get-tuple-element.87), channel_id=1, source_target_pairs={{16,0},{32,16},{48,32},{64,48},{80,64},{96,80},{112,96},{128,112},... | collective-permute-start | bytes 49160 | tf_op jit(solution)/shard_map/ppermute | solution.py:27
  20.0 24.7 %collective-permute-start.8 = (f32[1,16,256]{2,1,0:T(8,128)S(1)}, f32[1,16,256]{2,1,0:T(8,128)S(1)}, u32[]{:S(2)}, u32[]{:S(2)}) collective-permute-start(f32[1,16,256]{2,1,0:T(8,128)S(1)} %get-tuple-element.88), channel_id=1, source_target_pairs={{0,16},{16,32},{32,48},{48,64},{64,80},{80,96},{96,112},{112,128},... | collective-permute-start | bytes 49160 | tf_op jit(solution)/shard_map/ppermute | solution.py:24
  23.2 56.0 %collective-permute-start.5 = (f32[2,1,16,256]{3,2,1,0:T(8,128)S(1)}, f32[2,1,16,256]{3,2,1,0:T(8,128)S(1)}, u32[]{:S(2)}, u32[]{:S(2)}) collective-permute-start(f32[2,1,16,256]{3,2,1,0:T(8,128)S(1)} %get-tuple-element.64), channel_id=1, source_target_pairs={{16,0},{32,16},{48,32},{64,48},{80,64},{96,80},{112,96},{128,112},... | collective-permute-start | bytes 98312 | tf_op jit(solution)/shard_map/ppermute | solution.py:27
  28.4 50.7 %collective-permute-start.4 = (f32[2,1,16,256]{3,2,1,0:T(8,128)S(1)}, f32[2,1,16,256]{3,2,1,0:T(8,128)S(1)}, u32[]{:S(2)}, u32[]{:S(2)}) collective-permute-start(f32[2,1,16,256]{3,2,1,0:T(8,128)S(1)} %get-tuple-element.65), channel_id=1, source_target_pairs={{0,16},{16,32},{32,48},{48,64},{64,80},{80,96},{96,112},{112,128},... | collective-permute-start | bytes 98312 | tf_op jit(solution)/shard_map/ppermute | solution.py:24
  35.1 20.7 %all-to-all-start.1 = ((f32[16,1,144]{2,1,0:T(1,128)}), f32[16,1,144]{2,1,0:T(1,128)S(1)}, u32[]{:S(2)}, u32[]{:S(2)}) async-start(f32[16,1,144]{2,1,0:T(1,128)} %reshape.1544), calls=%async_computation.1 | async-start | bytes 32768 | tf_op jit(solution)/shard_map/all_to_all | solution.py:225
  44.7 34.4 %copy-start.5 = (f32[2,4,16,256]{3,2,1,0:T(8,128)S(1)}, f32[2,4,16,256]{3,2,1,0:T(8,128)}, u32[]{:S(2)}) copy-start(f32[2,4,16,256]{3,2,1,0:T(8,128)} %param.7) | copy-start | bytes 393220
  46.3 16.7 %collective-permute-start.10 = (f32[6,1,256]{2,1,0:T(1,128)S(1)}, f32[6,1,256]{2,1,0:T(1,128)S(1)}, u32[]{:S(2)}, u32[]{:S(2)}) collective-permute-start(f32[6,1,256]{2,1,0:T(1,128)S(1)} %get-tuple-element.83), channel_id=1, source_target_pairs={{0,1},{1,2},{2,3},{3,4},{4,5},{5,6},{6,7},{7,8},{8,9},{9,10},{10,1... | collective-permute-start | bytes 18440 | tf_op jit(solution)/shard_map/ppermute | solution.py:24
  50.6 14.4 %collective-permute-start.11 = (f32[6,1,256]{2,1,0:T(1,128)S(1)}, f32[6,1,256]{2,1,0:T(1,128)S(1)}, u32[]{:S(2)}, u32[]{:S(2)}) collective-permute-start(f32[6,1,256]{2,1,0:T(1,128)S(1)} %get-tuple-element.84), channel_id=1, source_target_pairs={{1,0},{2,1},{3,2},{4,3},{5,4},{6,5},{7,6},{8,7},{9,8},{10,9},{11,1... | collective-permute-start | bytes 18440 | tf_op jit(solution)/shard_map/ppermute | solution.py:27
  58.4 7.4 %collective-permute-start.1 = (f32[9,1,4,64]{3,2,0,1:T(4,128)S(1)}, f32[9,1,4,64]{3,2,0,1:T(4,128)S(1)}, u32[]{:S(2)}, u32[]{:S(2)}) collective-permute-start(f32[9,1,4,64]{3,2,0,1:T(4,128)S(1)} %copy.232), channel_id=1, source_target_pairs={{16,0},{32,16},{48,32},{64,48},{80,64},{96,80},{112,96},{128,112},... | collective-permute-start | bytes 27656 | tf_op jit(solution)/shard_map/ppermute | solution.py:27
  63.0 7.2 %collective-permute-start = (f32[9,1,4,64]{3,2,0,1:T(4,128)S(1)}, f32[9,1,4,64]{3,2,0,1:T(4,128)S(1)}, u32[]{:S(2)}, u32[]{:S(2)}) collective-permute-start(f32[9,1,4,64]{3,2,0,1:T(4,128)S(1)} %copy.232), channel_id=1, source_target_pairs={{0,16},{16,32},{32,48},{48,64},{64,80},{80,96},{96,112},{112,128},... | collective-permute-start | bytes 27656 | tf_op jit(solution)/shard_map/ppermute | solution.py:24
  70.2 17.0 %collective-permute-start.2 = (f32[9,3,1,64]{3,2,0,1:T(1,128)S(1)}, f32[9,3,1,64]{3,2,0,1:T(1,128)S(1)}, u32[]{:S(2)}, u32[]{:S(2)}) collective-permute-start(f32[9,3,1,64]{3,2,0,1:T(1,128)S(1)} %get-tuple-element.89), channel_id=1, source_target_pairs={{0,1},{1,2},{2,3},{3,4},{4,5},{5,6},{6,7},{7,8},{8,9},{9,10},{10,1... | collective-permute-start | bytes 20744 | tf_op jit(solution)/shard_map/ppermute | solution.py:24
  73.3 13.9 %collective-permute-start.3 = (f32[9,3,1,64]{3,2,0,1:T(1,128)S(1)}, f32[9,3,1,64]{3,2,0,1:T(1,128)S(1)}, u32[]{:S(2)}, u32[]{:S(2)}) collective-permute-start(f32[9,3,1,64]{3,2,0,1:T(1,128)S(1)} %get-tuple-element.90), channel_id=1, source_target_pairs={{1,0},{2,1},{3,2},{4,3},{5,4},{6,5},{7,6},{8,7},{9,8},{10,9},{11,1... | collective-permute-start | bytes 20744 | tf_op jit(solution)/shard_map/ppermute | solution.py:27
  79.2 8.1 %copy-start.4 = (f32[2,6,16,256]{3,2,1,0:T(8,128)}, f32[2,6,16,256]{3,2,1,0:T(8,128)S(1)}, u32[]{:S(2)}) copy-start(f32[2,6,16,256]{3,2,1,0:T(8,128)S(1)} %constant_dynamic-update-slice_fusion) | copy-start | bytes 589828
  80.4 27.2 %collective-permute-start.7 = (f32[2,6,1,256]{3,0,2,1:T(2,128)}, f32[2,6,1,256]{3,0,2,1:T(2,128)}, u32[]{:S(2)}, u32[]{:S(2)}) collective-permute-start(f32[2,6,1,256]{3,0,2,1:T(2,128)} %copy.317), channel_id=1, source_target_pairs={{1,0},{2,1},{3,2},{4,3},{5,4},{6,5},{7,6},{8,7},{9,8},{10,9},{11,1... | collective-permute-start | bytes 36872 | tf_op jit(solution)/shard_map/ppermute | solution.py:27
  82.7 25.7 %collective-permute-start.6 = (f32[2,6,1,256]{3,0,2,1:T(2,128)}, f32[2,6,1,256]{3,0,2,1:T(2,128)}, u32[]{:S(2)}, u32[]{:S(2)}) collective-permute-start(f32[2,6,1,256]{3,0,2,1:T(2,128)} %copy.316), channel_id=1, source_target_pairs={{0,1},{1,2},{2,3},{3,4},{4,5},{5,6},{6,7},{7,8},{8,9},{9,10},{10,1... | collective-permute-start | bytes 36872 | tf_op jit(solution)/shard_map/ppermute | solution.py:24
  114.7 0.7 copy-start.10
  115.3 0.6 copy-start.11
  115.3 0.9 copy-start.12
  115.3 1.1 copy-start
  115.3 1.1 copy-start.1
  115.3 1.1 copy-start.2
  115.4 1.1 copy-start.3
  115.4 1.1 copy-start.6
  115.4 1.1 copy-start.7
  115.4 1.1 copy-start.8
  115.5 1.1 copy-start.9
where the time goes:
time: 118 us; the launch traced here: 117 us
  starting transfers between devices  62.2 us (53%)
  local copies, waits for them, and re-layouts  31.1 us (26%)
  other arithmetic  18.2 us (15%)
  waiting for transfers between devices  4.48 us (4%)
  between operations  1.44 us (1%)
    ppermute x6, starting transfers between devices, padded_2(): lax.ppermute(lax.slice_in_dim(block, 0, width, axis=dim), axis, backward)  24.3 us
    ppermute x6, starting transfers between devices, padded_2(): lax.ppermute(lax.slice_in_dim(block, block.shape[dim] - width, None, axis...  18.1 us
    all_to_all x1, starting transfers between devices, local(): lax.all_to_all(wanted, 'gy', split_axis=0, concat_axis=0, tiled=True)  10.1 us
    all_to_all x1, starting transfers between devices, local(): lax.all_to_all(picked, 'gy', split_axis=1, concat_axis=1, tiled=True)  9.63 us
    slice x10, local copies, waits for them, and re-layouts, tensors(): entries = [field[number] for number in range(9)]  9.19 us
    unnamed x39, local copies, waits for them, and re-layouts  5.86 us
    squeeze x13, local copies, waits for them, and re-layouts, tensors(): entries = [field[number] for number in range(9)]  5.45 us
    ppermute x6, waiting for transfers between devices, padded_2(): lax.ppermute(lax.slice_in_dim(block, block.shape[dim] - width, None, axis...  4.46 us
  transfers between devices with their start and end apart: 14, of which 1 were waited for; matrix products, arithmetic and copies ran while one was open for 29% of the time, Pallas kernels for 0%

commit v1 on v0

v1 whole, which is shorter than its diff:
```python
import jax
import jax.numpy as jnp
from jax import lax
from jax.experimental import pallas as pl
from jax.experimental.pallas import tpu as pltpu
from jax.sharding import PartitionSpec as P

sigma_fiber = 1.0
sigma_cross = 0.3
time_step = 0.1
excite_gain = 8.0
excite_level = 0.15
stretch_gain = 10.0
stretch_reversal = 0.6
recover_rate = 0.5

MESH = pl.DeviceIdType.MESH
F32 = jnp.float32
BF16 = jnp.bfloat16

ROWS = 104
LAST = 96


def sin_cos(angle):
    half = 0.5 * angle
    sq = half * half
    s = -2.5052108e-08
    for c in (2.7557319e-06, -1.9841270e-04, 8.3333333e-03, -1.6666667e-01, 1.0):
        s = s * sq + c
    s = s * half
    c2 = 2.0876757e-09
    for c in (-2.7557319e-07, 2.4801587e-05, -1.3888889e-03, 4.1666667e-02, -0.5, 1.0):
        c2 = c2 * sq + c
    return 2.0 * s * c2, 1.0 - 2.0 * s * s


def fibers(azimuth, elevation):
    sin_a, cos_a = sin_cos(azimuth)
    sin_e, cos_e = sin_cos(elevation)
    return cos_a * cos_e, sin_a * cos_e, sin_e


def tensor_rows(f, fiber, want_stretch):
    def el(i, j):
        return f[3 * (i % 3) + j % 3]

    cof = [
        [el(i + 1, j + 1) * el(i + 2, j + 2) - el(i + 1, j + 2) * el(i + 2, j + 1) for j in range(3)]
        for i in range(3)
    ]
    det = el(0, 0) * cof[0][0] + el(0, 1) * cof[0][1] + el(0, 2) * cof[0][2]
    inv = 1.0 / det
    scale = inv * inv
    stretch = None
    if want_stretch:
        st = [el(i, 0) * fiber[0] + el(i, 1) * fiber[1] + el(i, 2) * fiber[2] for i in range(3)]
        stretch = jnp.sqrt(st[0] * st[0] + st[1] * st[1] + st[2] * st[2])
    pulled = [cof[0][i] * fiber[0] + cof[1][i] * fiber[1] + cof[2][i] * fiber[2] for i in range(3)]
    out = []
    for a, b in ((0, 0), (1, 1), (2, 2), (0, 1), (0, 2), (1, 2)):
        metric = cof[0][a] * cof[0][b] + cof[1][a] * cof[1][b] + cof[2][a] * cof[2][b]
        out.append(
            (sigma_cross * metric + (sigma_fiber - sigma_cross) * pulled[a] * pulled[b]) * scale
        )
    return out, stretch


def kernel(
    n_x, n_y, split, order,
    pot_in, rec_in, ang_in, def_in, slot_in, pot_out, rec_out,
    pot, rec, ang, dfm, slot, ag8, ag1, ysend, yrecv, srecv, xpot, xang, xcor, s8, s1,
    fib, crs, fine, con, stretch, vh, onew, onev,
    in_sem, out_sem, ag_send, ag_recv, y_send, y_recv, x_send, x_recv, c_send, c_recv,
):
    gx = lax.axis_index("gx")
    gy = lax.axis_index("gy")
    up_x, down_x = lax.rem(gx + 1, n_x), lax.rem(gx + n_x - 1, n_x)
    up_y, down_y = lax.rem(gy + 1, n_y), lax.rem(gy + n_y - 1, n_y)
    outer, inner = split
    my_o, my_i = lax.div(gy, inner), lax.rem(gy, inner)

    def peer(number):
        step_o, step_i = number // inner, number % inner
        return lax.rem(my_o + step_o, outer) * inner + lax.rem(my_i + step_i, inner)

    barrier = pltpu.get_barrier_semaphore()
    for number in order:
        pl.semaphore_signal(barrier, inc=1, device_id=(gx, peer(number)), device_id_type=MESH)
    for other in (up_x, down_x):
        pl.semaphore_signal(barrier, inc=1, device_id=(other, gy), device_id_type=MESH)

    loads = [
        pltpu.make_async_copy(src, dst, in_sem.at[i])
        for i, (src, dst) in enumerate(
            ((def_in, dfm), (slot_in, slot), (pot_in, pot), (ang_in, ang), (rec_in, rec))
        )
    ]
    for load in loads:
        load.start()
    loads[0].wait()
    ag8[0] = dfm[0:8]
    ag1[0] = dfm[8:9]
    loads[1].wait()
    loads[2].wait()
    loads[3].wait()
    for side, row in ((0, 0), (1, 15)):
        ysend[side, 0:4] = pot[:, row, :]
        ysend[side, 4:8] = ang[0, :, row, :]
        ysend[side, 8:12] = ang[1, :, row, :]

    pl.semaphore_wait(barrier, n_y + 1)

    sends = []

    def send(src, dst, send_sem, recv_sem, device):
        copy = pltpu.make_async_remote_copy(
            src_ref=src, dst_ref=dst, send_sem=send_sem, recv_sem=recv_sem,
            device_id=device, device_id_type=MESH,
        )
        copy.start()
        sends.append(copy)
        return copy

    gathers = []
    for number in order:
        device = (gx, peer(number))
        gathers.append(send(ag8.at[0], ag8.at[number], ag_send.at[0, number], ag_recv.at[0, number], device))
        gathers.append(send(ag1.at[0], ag1.at[number], ag_send.at[1, number], ag_recv.at[1, number], device))
    halos = []
    for side, device in ((0, (gx, down_y)), (1, (gx, up_y))):
        halos.append(send(slot, srecv.at[1 - side], y_send.at[0, side], y_recv.at[0, side], device))
        halos.append(send(ysend.at[side], yrecv.at[1 - side], y_send.at[1, side], y_recv.at[1, side], device))
    planes = []
    for side, device in ((0, (down_x, gy)), (1, (up_x, gy))):
        planes.append(send(pot.at[3 * side], xpot.at[1 - side], x_send.at[0, side], x_recv.at[0, side], device))
        for which in range(2):
            planes.append(
                send(
                    ang.at[which, 3 * side], xang.at[1 - side, which],
                    x_send.at[1 + which, side], x_recv.at[1 + which, side], device,
                )
            )

    loads[4].wait()
    for x in range(4):
        v, w = pot[x], rec[x]
        onew[x] = w + time_step * recover_rate * (
            -w - excite_gain * v * (v - excite_level - 1.0)
        )
        f = fibers(ang[0, x], ang[1, x])
        for i in range(3):
            fib[i, 16 * (x + 1) : 16 * (x + 2)] = f[i]
    rec_store = pltpu.make_async_copy(onew, rec_out, out_sem.at[0])
    rec_store.start()

    k_iota = lax.broadcasted_iota(jnp.int32, (128, 256), 0) & 63
    z_iota = lax.broadcasted_iota(jnp.int32, (128, 256), 1)
    place = jnp.clip((z_iota.astype(F32) + 0.5) * 0.25 - 0.5, 0.0, 63.0)
    hat = jnp.maximum(1.0 - jnp.abs(place - k_iota.astype(F32)), 0.0).astype(BF16)

    for copy in halos:
        copy.wait_recv()
    corners = []
    for side, device in ((0, (down_x, gy)), (1, (up_x, gy))):
        for which in range(2):
            corners.append(
                send(
                    yrecv.at[which, 0:8], xcor.at[1 - side, which],
                    x_send.at[3 + which, side], x_recv.at[3 + which, side], device,
                )
            )
    azimuth = jnp.concatenate([yrecv[0, 4:8], yrecv[1, 4:8]], axis=0)
    elevation = jnp.concatenate([yrecv[0, 8:12], yrecv[1, 8:12]], axis=0)
    f = fibers(azimuth, elevation)
    for i in range(3):
        fib[i, LAST : LAST + 8] = f[i]

    mine = slot[...]
    below = jnp.where(gy == 0, mine[0:1], srecv[0, 3:4])
    above = jnp.where(gy == n_y - 1, mine[3:4], srecv[1, 0:1])
    wanted = jnp.concatenate(
        [piece for row in (below, mine[0:1], mine[1:2], mine[2:3], mine[3:4], above) for piece in (row, row)],
        axis=1,
    )
    local = wanted & 255
    holder = (wanted >> 8) & (n_y - 1)
    from_o = (my_o - (holder >> (inner.bit_length() - 1))) & (outer - 1)
    from_i = (my_i - (holder & (inner - 1))) & (inner - 1)
    source = from_o * inner + from_i
    hot = jnp.where(
        lax.broadcasted_iota(jnp.int32, (256, 768), 0) == local, 1.0, 0.0
    ).astype(BF16)

    for copy in gathers:
        copy.wait_recv()
    d8 = ag8[...].reshape(n_y * 8, 256)
    d1 = ag1[...].reshape(n_y, 256)
    both = jnp.concatenate([d8, d1], axis=0)
    high = both.astype(BF16)
    low = (both - high.astype(F32)).astype(BF16)
    chosen = jnp.dot(high, hot, preferred_element_type=F32) + jnp.dot(
        low, hot, preferred_element_type=F32
    )
    total = jnp.zeros((8, 768), F32)
    for number in range(n_y):
        total = total + jnp.where(source == number, chosen[8 * number : 8 * number + 8], 0.0)
    s8[0] = total
    last = chosen[8 * n_y : 9 * n_y]
    s1[0] = jnp.sum(
        jnp.where(lax.broadcasted_iota(jnp.int32, (n_y, 768), 0) == source, last, 0.0),
        axis=0, keepdims=True,
    )
    coarse = []
    for side, device in ((0, (down_x, gy)), (1, (up_x, gy))):
        coarse.append(send(s8.at[0], s8.at[2 - side], c_send.at[0, side], c_recv.at[0, side], device))
        coarse.append(send(s1.at[0], s1.at[2 - side], c_send.at[1, side], c_recv.at[1, side], device))

    for copy in planes:
        copy.wait_recv()
    for side, start in ((0, 0), (1, 80)):
        f = fibers(xang[side, 0], xang[side, 1])
        for i in range(3):
            fib[i, start : start + 16] = f[i]
    for copy in corners:
        copy.wait_recv()
    first_x, last_x, first_y, last_y = gx == 0, gx == n_x - 1, gy == 0, gy == n_y - 1
    volt = [jnp.where(first_x, pot[0], xpot[0])]
    volt += [pot[x] for x in range(4)]
    volt += [jnp.where(last_x, pot[3], xpot[1])]
    for which, row, outside in ((0, 0, first_y), (1, 15, last_y)):
        ring = [
            jnp.where(first_x, yrecv[which, 0:1], xcor[0, which, 3:4]),
            yrecv[which, 0:1], yrecv[which, 1:2], yrecv[which, 2:3], yrecv[which, 3:4],
            jnp.where(last_x, yrecv[which, 3:4], xcor[1, which, 0:1]),
        ]
        for p in range(6):
            vh[which, p : p + 1] = jnp.where(outside, volt[p][row : row + 1], ring[p])

    for copy in coarse:
        copy.wait_recv()
    sub = lax.broadcasted_iota(jnp.int32, (8, 128), 0)

    def hat_rows(start, element):
        t = (sub.astype(F32) + (start + 0.5)) * 0.25 - 0.5
        return jnp.maximum(1.0 - jnp.abs(t - element), 0.0)

    tile0 = [hat_rows(0, e - 1) for e in range(4)]
    tile1 = [hat_rows(8, e + 1) for e in range(4)]
    t = ((sub & 3).astype(F32) + 0.5) * 0.25 - 0.5
    cross = [jnp.maximum(1.0 - jnp.abs(t - (e - 1)), 0.0) for e in range(3)]
    low_half = sub < 4
    for k in range(9):
        tiles0, tiles1, beside = [], [], []
        for which in (1, 0, 2):
            rows = []
            for e in range(6):
                lanes = slice(128 * e, 128 * e + 128)
                row = s8[which, k : k + 1, lanes] if k < 8 else s1[which, :, lanes]
                if which == 1:
                    own = s8[0, k : k + 1, lanes] if k < 8 else s1[0, :, lanes]
                    row = jnp.where(first_x, own, row)
                if which == 2:
                    own = s8[0, k : k + 1, lanes] if k < 8 else s1[0, :, lanes]
                    row = jnp.where(last_x, own, row)
                rows.append(jnp.broadcast_to(row, (8, 128)))
            tiles0.append(sum(tile0[i] * rows[i] for i in range(4)))
            tiles1.append(sum(tile1[i] * rows[i + 2] for i in range(4)))
            beside.append(
                jnp.where(low_half, 0.625 * rows[0] + 0.375 * rows[1], 0.625 * rows[5] + 0.375 * rows[4])
            )
        base = ROWS * k
        for p, (a, b, c) in enumerate(
            (
                (0.625, 0.375, 0.0), (0.375, 0.625, 0.0), (0.125, 0.875, 0.0),
                (0.0, 0.875, 0.125), (0.0, 0.625, 0.375), (0.0, 0.375, 0.625),
            )
        ):
            for half, tiles in ((0, tiles0), (8, tiles1)):
                if c == 0.0:
                    value = a * tiles[0] + b * tiles[1]
                else:
                    value = b * tiles[1] + c * tiles[2]
                crs[base + 16 * p + half : base + 16 * p + half + 8] = value
        crs[base + LAST : base + LAST + 8] = (
            cross[0] * beside[0] + cross[1] * beside[1] + cross[2] * beside[2]
        )
    c = crs[...]
    rest = c - c.astype(BF16).astype(F32)
    left = lax.broadcasted_iota(jnp.int32, c.shape, 1) < 64
    fine[...] = jnp.dot(
        jnp.where(left, c, rest).astype(BF16), hat, preferred_element_type=F32
    )

    for tile in range(13):
        at = 8 * tile
        f = [fine[ROWS * k + at : ROWS * k + at + 8] for k in range(9)]
        fiber = [fib[i, at : at + 8] for i in range(3)]
        own = 2 <= tile < 10
        d, s = tensor_rows(f, fiber, own)
        for i in range(6):
            con[i, at : at + 8] = d[i]
        if own:
            stretch[at - 16 : at - 8] = s

    row_iota = lax.broadcasted_iota(jnp.int32, (16, 256), 0)
    lane = lax.broadcasted_iota(jnp.int32, (16, 256), 1)

    def from_below(a, edge):
        return jnp.where(row_iota == 0, edge, pltpu.roll(a, 1, 0))

    def from_above(a, edge):
        return jnp.where(row_iota == 15, edge, pltpu.roll(a, 15, 0))

    def z_slope(v):
        n = v.shape[0]
        at = lax.broadcasted_iota(jnp.int32, (n, 256), 1)
        after = jnp.where(at == 255, v, pltpu.roll(v, 255, 1))
        before = jnp.where(at == 0, v, pltpu.roll(v, 1, 1))
        return after - before

    def flux(d1, step, d2, s2, d3, s3):
        return 0.5 * (d1 * step + 0.25 * (d2 * s2 + d3 * s3))

    XX, YY, ZZ, XY, XZ, YZ = range(6)
    slope_y = [from_above(volt[p], vh[1, p : p + 1]) - from_below(volt[p], vh[0, p : p + 1]) for p in range(6)]
    slope_z = [z_slope(volt[p]) for p in range(6)]
    edge_z = [z_slope(vh[which]) for which in range(2)]

    def plane(i, p):
        return con[i, 16 * p : 16 * p + 16]

    flux_x = []
    for p in range(5):
        value = flux(
            plane(XX, p) + plane(XX, p + 1), volt[p + 1] - volt[p],
            plane(XY, p) + plane(XY, p + 1), slope_y[p] + slope_y[p + 1],
            plane(XZ, p) + plane(XZ, p + 1), slope_z[p] + slope_z[p + 1],
        )
        if p == 0:
            value = jnp.where(first_x, 0.0, value)
        if p == 4:
            value = jnp.where(last_x, 0.0, value)
        flux_x.append(value)
    for x in range(4):
        p = x + 1
        v = volt[p]
        slope_x = volt[p + 1] - volt[p - 1]
        d_xy, d_yy, d_yz = plane(XY, p), plane(YY, p), plane(YZ, p)
        faces = []
        for which, shift in ((0, from_below), (1, from_above)):
            row = LAST + 4 * which + x
            step = shift(v, vh[which, p : p + 1])
            step = v - step if which == 0 else step - v
            faces.append(
                flux(
                    d_yy + shift(d_yy, con[YY, row : row + 1]), step,
                    d_xy + shift(d_xy, con[XY, row : row + 1]),
                    slope_x + shift(slope_x, vh[which, p + 1 : p + 2] - vh[which, p - 1 : p]),
                    d_yz + shift(d_yz, con[YZ, row : row + 1]),
                    slope_z[p] + shift(slope_z[p], edge_z[which][p : p + 1]),
                )
            )
        faces[0] = jnp.where((row_iota == 0) & first_y, 0.0, faces[0])
        faces[1] = jnp.where((row_iota == 15) & last_y, 0.0, faces[1])

        def onward(a):
            return pltpu.roll(a, 255, 1)

        d_xz, d_zz = plane(XZ, p), plane(ZZ, p)
        upper = flux(
            d_zz + onward(d_zz), onward(v) - v,
            d_xz + onward(d_xz), slope_x + onward(slope_x),
            d_yz + onward(d_yz), slope_y[p] + onward(slope_y[p]),
        )
        upper = jnp.where(lane == 255, 0.0, upper)
        divergent = (
            flux_x[p] - flux_x[p - 1] + (faces[1] - faces[0]) + (upper - pltpu.roll(upper, 1, 1))
        )
        w = rec[x]
        current = excite_gain * v * (v - excite_level) * (v - 1.0) + v * w
        current = current + stretch_gain * jnp.maximum(stretch[16 * x : 16 * x + 16] - 1.0, 0.0) * (
            v - stretch_reversal
        )
        onev[x] = v + time_step * (divergent - current)
    pot_store = pltpu.make_async_copy(onev, pot_out, out_sem.at[1])
    pot_store.start()
    for copy in sends:
        copy.wait_send()
    rec_store.wait()
    pot_store.wait()


def make_local(n_x, n_y):
    split = (4, 4) if n_y == 16 else (n_y // 2, 2)
    outer, inner = split

    def reach(number):
        o, i = number // inner, number % inner
        return min(o, outer - o) + 2 * min(i, inner - i)

    order = sorted(range(1, n_y), key=lambda number: -reach(number))

    def local(potential, recovery, fiber_angles, deform, elem_slot):
        anywhere = pl.BlockSpec(memory_space=pl.ANY)
        cells = (4, 16, 256)
        dma = pltpu.SemaphoreType.DMA
        call = pl.pallas_call(
            lambda *refs: kernel(n_x, n_y, split, order, *refs),
            out_shape=(jax.ShapeDtypeStruct(cells, F32),) * 2,
            in_specs=[anywhere] * 5,
            out_specs=(anywhere, anywhere),
            scratch_shapes=[
                pltpu.VMEM(cells, F32),
                pltpu.VMEM(cells, F32),
                pltpu.VMEM((2,) + cells, F32),
                pltpu.VMEM((9, 256), F32),
                pltpu.VMEM((4, 64), jnp.int32),
                pltpu.VMEM((n_y, 8, 256), F32),
                pltpu.VMEM((n_y, 1, 256), F32),
                pltpu.VMEM((2, 16, 256), F32),
                pltpu.VMEM((2, 16, 256), F32),
                pltpu.VMEM((2, 4, 64), jnp.int32),
                pltpu.VMEM((2, 16, 256), F32),
                pltpu.VMEM((2, 2, 16, 256), F32),
                pltpu.VMEM((2, 2, 8, 256), F32),
                pltpu.VMEM((3, 8, 768), F32),
                pltpu.VMEM((3, 1, 768), F32),
                pltpu.VMEM((3, ROWS, 256), F32),
                pltpu.VMEM((9 * ROWS, 128), F32),
                pltpu.VMEM((9 * ROWS, 256), F32),
                pltpu.VMEM((6, ROWS, 256), F32),
                pltpu.VMEM((64, 256), F32),
                pltpu.VMEM((2, 8, 256), F32),
                pltpu.VMEM(cells, F32),
                pltpu.VMEM(cells, F32),
                dma((5,)),
                dma((2,)),
                dma((2, n_y)),
                dma((2, n_y)),
                dma((2, 2)),
                dma((2, 2)),
                dma((5, 2)),
                dma((5, 2)),
                dma((2, 2)),
                dma((2, 2)),
            ],
            compiler_params=pltpu.CompilerParams(collective_id=0, has_side_effects=True),
            name="step",
        )
        return call(potential, recovery, fiber_angles, deform, elem_slot.reshape(4, 64))

    return local


def solution(mesh):
    placed = (
        P("gx", "gy", None),
        P("gx", "gy", None),
        P(None, "gx", "gy", None),
        P(None, ("gx", "gy")),
        P("gx", "gy", None),
    )
    return jax.shard_map(
        make_local(mesh.shape["gx"], mesh.shape["gy"]),
        mesh=mesh,
        in_specs=placed,
        out_specs=(P("gx", "gy", None), P("gx", "gy", None)),
        check_vma=False,
    )
```

time: 118 us -> 29.4 us (0.25)
  the two profiles are of different devices: /device:TPU:262 before, /device:TPU:2 now
where the time goes in v1:
time: 29.4 us; the launch traced here: 29.2 us
  Pallas kernels  26.5 us (90%)
  local copies, waits for them, and re-layouts  2.14 us (7%)
  between operations  0.65 us (2%)
    pallas_call x1, Pallas kernels, local(): call(potential, recovery, fiber_angles, deform, elem_slot.reshape(4, 64))  26.5 us
    unnamed x4, local copies, waits for them, and re-layouts  2.14 us

profile of v1, /device:TPU:2, one launch (start us, length us, event | category | flops | bytes accessed | tf_op | source)
XLA Modules:
  0.0 29.2 jit_solution(15385005906723328163)
XLA Ops:
  0.6 26.5 %step.1 = (f32[4,16,256]{2,1,0:T(8,128)}, f32[4,16,256]{2,1,0:T(8,128)}) custom-call(f32[4,16,256]{2,1,0:T(8,128)} %refs_0_.1, f32[4,16,256]{2,1,0:T(8,128)} %refs_1_.1, f32[2,4,16,256]{3,2,1,0:T(8,128)} %refs_2_.1, f32[9,256]{1,0:T(8,128)} %refs_3_.1, s32[4,64]{1,0:T(4,128)} %bitcast.1), custom_call_target="tpu_custom_call" | custom-call | tf_op jit(solution)/shard_map/step/pallas_call | solution.py:451
  27.1 0.0 copy-start
  27.1 1.5 %copy.9 = f32[4,16,256]{2,1,0:T(8,128)} copy(f32[4,16,256]{2,1,0:T(8,128)} %get-tuple-element.4) | data formatting | bytes 131072
  28.6 0.0 copy-done
  28.6 0.6 %copy.10 = f32[4,16,256]{2,1,0:T(8,128)} copy(f32[4,16,256]{2,1,0:T(8,128)S(1)} %copy-done) | data formatting | bytes 131072
Async XLA Ops:
  27.1 1.5 %copy-start = (f32[4,16,256]{2,1,0:T(8,128)S(1)}, f32[4,16,256]{2,1,0:T(8,128)}, u32[]{:S(2)}) copy-start(f32[4,16,256]{2,1,0:T(8,128)} %get-tuple-element.5) | copy-start | bytes 196612

commit v2 on v1

--- a/solution.py
+++ b/solution.py
@@ -75,20 +75,15 @@
 ):
     gx = lax.axis_index("gx")
     gy = lax.axis_index("gy")
-    up_x, down_x = lax.rem(gx + 1, n_x), lax.rem(gx + n_x - 1, n_x)
-    up_y, down_y = lax.rem(gy + 1, n_y), lax.rem(gy + n_y - 1, n_y)
+    first_x, last_x, first_y, last_y = gx == 0, gx == n_x - 1, gy == 0, gy == n_y - 1
+    x_sides = ((jnp.logical_not(first_x), (gx - 1, gy), 0), (jnp.logical_not(last_x), (gx + 1, gy), 3))
+    y_sides = ((jnp.logical_not(first_y), (gx, gy - 1), 0), (jnp.logical_not(last_y), (gx, gy + 1), 15))
     outer, inner = split
     my_o, my_i = lax.div(gy, inner), lax.rem(gy, inner)
 
     def peer(number):
         step_o, step_i = number // inner, number % inner
         return lax.rem(my_o + step_o, outer) * inner + lax.rem(my_i + step_i, inner)
-
-    barrier = pltpu.get_barrier_semaphore()
-    for number in order:
-        pl.semaphore_signal(barrier, inc=1, device_id=(gx, peer(number)), device_id_type=MESH)
-    for other in (up_x, down_x):
-        pl.semaphore_signal(barrier, inc=1, device_id=(other, gy), device_id_type=MESH)
 
     loads = [
         pltpu.make_async_copy(src, dst, in_sem.at[i])
@@ -96,51 +91,104 @@
             ((def_in, dfm), (slot_in, slot), (pot_in, pot), (ang_in, ang), (rec_in, rec))
         )
     ]
-    for load in loads:
+    loads[0].start()
+    barrier = pltpu.get_barrier_semaphore()
+    for number in order:
+        pl.semaphore_signal(barrier, inc=1, device_id=(gx, peer(number)), device_id_type=MESH)
+    for there, device, _ in x_sides:
+
+        @pl.when(there)
+        def _(device=device):
+            pl.semaphore_signal(barrier, inc=1, device_id=device, device_id_type=MESH)
+
+    for load in loads[1:]:
         load.start()
     loads[0].wait()
     ag8[0] = dfm[0:8]
     ag1[0] = dfm[8:9]
+    pl.semaphore_wait(barrier, n_y - 1 + jnp.where(first_x, 0, 1) + jnp.where(last_x, 0, 1))
+
+    def remote(src, dst, send_sem, recv_sem, device):
+        return pltpu.make_async_remote_copy(
+            src_ref=src, dst_ref=dst, send_sem=send_sem, recv_sem=recv_sem,
+            device_id=device, device_id_type=MESH,
+        )
+
+    def send(there, copies):
+        @pl.when(there)
+        def _():
+            for copy in copies:
+                copy.start()
+
+    def arrived(there, copies, otherwise):
+        @pl.when(there)
+        def _():
+            for copy in copies:
+                copy.wait_recv()
+
+        @pl.when(jnp.logical_not(there))
+        def _():
+            otherwise()
+
+    def sent(there, copies):
+        @pl.when(there)
+        def _():
+            for copy in copies:
+                copy.wait_send()
+
+    gathers = []
+    for number in order:
+        device = (gx, peer(number))
+        gathers += [
+            remote(ag8.at[0], ag8.at[number], ag_send.at[0, number], ag_recv.at[0, number], device),
+            remote(ag1.at[0], ag1.at[number], ag_send.at[1, number], ag_recv.at[1, number], device),
+        ]
+        for copy in gathers[-2:]:
+            copy.start()
     loads[1].wait()
     loads[2].wait()
     loads[3].wait()
-    for side, row in ((0, 0), (1, 15)):
+    halos, planes, corners, coarse = [], [], [], []
+    for side, (there, device, row) in enumerate(y_sides):
         ysend[side, 0:4] = pot[:, row, :]
         ysend[side, 4:8] = ang[0, :, row, :]
         ysend[side, 8:12] = ang[1, :, row, :]
-
-    pl.semaphore_wait(barrier, n_y + 1)
-
-    sends = []
-
-    def send(src, dst, send_sem, recv_sem, device):
-        copy = pltpu.make_async_remote_copy(
-            src_ref=src, dst_ref=dst, send_sem=send_sem, recv_sem=recv_sem,
-            device_id=device, device_id_type=MESH,
-        )
-        copy.start()
-        sends.append(copy)
-        return copy
-
-    gathers = []
-    for number in order:
-        device = (gx, peer(number))
-        gathers.append(send(ag8.at[0], ag8.at[number], ag_send.at[0, number], ag_recv.at[0, number], device))
-        gathers.append(send(ag1.at[0], ag1.at[number], ag_send.at[1, number], ag_recv.at[1, number], device))
-    halos = []
-    for side, device in ((0, (gx, down_y)), (1, (gx, up_y))):
-        halos.append(send(slot, srecv.at[1 - side], y_send.at[0, side], y_recv.at[0, side], device))
-        halos.append(send(ysend.at[side], yrecv.at[1 - side], y_send.at[1, side], y_recv.at[1, side], device))
-    planes = []
-    for side, device in ((0, (down_x, gy)), (1, (up_x, gy))):
-        planes.append(send(pot.at[3 * side], xpot.at[1 - side], x_send.at[0, side], x_recv.at[0, side], device))
-        for which in range(2):
-            planes.append(
-                send(
-                    ang.at[which, 3 * side], xang.at[1 - side, which],
-                    x_send.at[1 + which, side], x_recv.at[1 + which, side], device,
+        halos.append(
+            [
+                remote(slot, srecv.at[1 - side], y_send.at[0, side], y_recv.at[0, 1 - side], device),
+                remote(ysend.at[side], yrecv.at[1 - side], y_send.at[1, side], y_recv.at[1, 1 - side], device),
+            ]
+        )
+    for side, (there, device, x) in enumerate(x_sides):
+        planes.append(
+            [remote(pot.at[x], xpot.at[1 - side], x_send.at[0, side], x_recv.at[0, 1 - side], device)]
+            + [
+                remote(
+                    ang.at[which, x], xang.at[1 - side, which],
+                    x_send.at[1 + which, side], x_recv.at[1 + which, 1 - side], device,
                 )
-            )
+                for which in range(2)
+            ]
+        )
+        corners.append(
+            [
+                remote(
+                    yrecv.at[which, 0:8], xcor.at[1 - side, which],
+                    x_send.at[3 + which, side], x_recv.at[3 + which, 1 - side], device,
+                )
+                for which in range(2)
+            ]
+        )
+        coarse.append(
+            [
+                remote(s8.at[0], s8.at[2 - side], c_send.at[0, side], c_recv.at[0, 1 - side], device),
+                remote(s1.at[0], s1.at[2 - side], c_send.at[1, side], c_recv.at[1, 1 - side], device),
+            ]
+        )
+    for (there, _, _), copies in zip(x_sides, planes):
+        send(there, copies)
+    for (there, _, _), copies in zip(y_sides, halos):
+        send(there, copies)
 
     loads[4].wait()
     for x in range(4):
@@ -159,17 +207,15 @@
     place = jnp.clip((z_iota.astype(F32) + 0.5) * 0.25 - 0.5, 0.0, 63.0)
     hat = jnp.maximum(1.0 - jnp.abs(place - k_iota.astype(F32)), 0.0).astype(BF16)
 
-    for copy in halos:
-        copy.wait_recv()
-    corners = []
-    for side, device in ((0, (down_x, gy)), (1, (up_x, gy))):
-        for which in range(2):
-            corners.append(
-                send(
-                    yrecv.at[which, 0:8], xcor.at[1 - side, which],
-                    x_send.at[3 + which, side], x_recv.at[3 + which, side], device,
-                )
-            )
+    for side, (there, _, row) in enumerate(y_sides):
+
+        def own_row(side=side, row=row):
+            yrecv[side, 0:12] = ysend[side, 0:12]
+            srecv[side] = slot[...]
+
+        arrived(there, halos[1 - side], own_row)
+    for (there, _, _), copies in zip(x_sides, corners):
+        send(there, copies)
     azimuth = jnp.concatenate([yrecv[0, 4:8], yrecv[1, 4:8]], axis=0)
     elevation = jnp.concatenate([yrecv[0, 8:12], yrecv[1, 8:12]], axis=0)
     f = fibers(azimuth, elevation)
@@ -177,8 +223,8 @@
         fib[i, LAST : LAST + 8] = f[i]
 
     mine = slot[...]
-    below = jnp.where(gy == 0, mine[0:1], srecv[0, 3:4])
-    above = jnp.where(gy == n_y - 1, mine[3:4], srecv[1, 0:1])
+    below = jnp.where(first_y, mine[0:1], srecv[0, 3:4])
+    above = jnp.where(last_y, mine[3:4], srecv[1, 0:1])
     wanted = jnp.concatenate(
         [piece for row in (below, mine[0:1], mine[1:2], mine[2:3], mine[3:4], above) for piece in (row, row)],
         axis=1,
@@ -211,34 +257,48 @@
         jnp.where(lax.broadcasted_iota(jnp.int32, (n_y, 768), 0) == source, last, 0.0),
         axis=0, keepdims=True,
     )
-    coarse = []
-    for side, device in ((0, (down_x, gy)), (1, (up_x, gy))):
-        coarse.append(send(s8.at[0], s8.at[2 - side], c_send.at[0, side], c_recv.at[0, side], device))
-        coarse.append(send(s1.at[0], s1.at[2 - side], c_send.at[1, side], c_recv.at[1, side], device))
-
-    for copy in planes:
-        copy.wait_recv()
+    for i in range(2):
+        for (there, _, _), copies in zip(x_sides, coarse):
+            send(there, copies[i : i + 1])
+
+    for side, (there, _, x) in enumerate(x_sides):
+
+        def own_plane(side=side, x=x):
+            xpot[side] = pot[x]
+            xang[side] = ang[:, x]
+            for which in range(2):
+                for i in (0, 3):
+                    xcor[side, which, i : i + 1] = yrecv[which, x : x + 1]
+
+        arrived(there, planes[1 - side] + corners[1 - side], own_plane)
     for side, start in ((0, 0), (1, 80)):
         f = fibers(xang[side, 0], xang[side, 1])
         for i in range(3):
             fib[i, start : start + 16] = f[i]
-    for copy in corners:
-        copy.wait_recv()
-    first_x, last_x, first_y, last_y = gx == 0, gx == n_x - 1, gy == 0, gy == n_y - 1
-    volt = [jnp.where(first_x, pot[0], xpot[0])]
-    volt += [pot[x] for x in range(4)]
-    volt += [jnp.where(last_x, pot[3], xpot[1])]
+    volt = [xpot[0]] + [pot[x] for x in range(4)] + [xpot[1]]
     for which, row, outside in ((0, 0, first_y), (1, 15, last_y)):
         ring = [
-            jnp.where(first_x, yrecv[which, 0:1], xcor[0, which, 3:4]),
+            xcor[0, which, 3:4],
             yrecv[which, 0:1], yrecv[which, 1:2], yrecv[which, 2:3], yrecv[which, 3:4],
-            jnp.where(last_x, yrecv[which, 3:4], xcor[1, which, 0:1]),
+            xcor[1, which, 0:1],
         ]
         for p in range(6):
             vh[which, p : p + 1] = jnp.where(outside, volt[p][row : row + 1], ring[p])
 
-    for copy in coarse:
-        copy.wait_recv()
+    for copy in gathers:
+        copy.wait_send()
+    for (there, _, _), copies in zip(y_sides, halos):
+        sent(there, copies)
+    for (there, _, _), first, second in zip(x_sides, planes, corners):
+        sent(there, first + second)
+
+    for side, (there, _, _) in enumerate(x_sides):
+
+        def own_elements(side=side):
+            s8[1 + side] = s8[0]
+            s1[1 + side] = s1[0]
+
+        arrived(there, coarse[1 - side], own_elements)
     sub = lax.broadcasted_iota(jnp.int32, (8, 128), 0)
 
     def hat_rows(start, element):
@@ -257,12 +317,6 @@
             for e in range(6):
                 lanes = slice(128 * e, 128 * e + 128)
                 row = s8[which, k : k + 1, lanes] if k < 8 else s1[which, :, lanes]
-                if which == 1:
-                    own = s8[0, k : k + 1, lanes] if k < 8 else s1[0, :, lanes]
-                    row = jnp.where(first_x, own, row)
-                if which == 2:
-                    own = s8[0, k : k + 1, lanes] if k < 8 else s1[0, :, lanes]
-                    row = jnp.where(last_x, own, row)
                 rows.append(jnp.broadcast_to(row, (8, 128)))
             tiles0.append(sum(tile0[i] * rows[i] for i in range(4)))
             tiles1.append(sum(tile1[i] * rows[i + 2] for i in range(4)))
@@ -385,8 +439,8 @@
         onev[x] = v + time_step * (divergent - current)
     pot_store = pltpu.make_async_copy(onev, pot_out, out_sem.at[1])
     pot_store.start()
-    for copy in sends:
-        copy.wait_send()
+    for (there, _, _), copies in zip(x_sides, coarse):
+        sent(there, copies)
     rec_store.wait()
     pot_store.wait()
 

time: 29.4 us -> 26.3 us (0.89)
  the two profiles are of different devices: /device:TPU:2 before, /device:TPU:217 now
where the time goes in v2:
time: 26.3 us; the launch traced here: 26.1 us
  Pallas kernels  23.3 us (89%)
  local copies, waits for them, and re-layouts  2.14 us (8%)
  between operations  0.65 us (2%)
    pallas_call x1, Pallas kernels, local(): call(potential, recovery, fiber_angles, deform, elem_slot.reshape(4, 64))  23.3 us
    unnamed x4, local copies, waits for them, and re-layouts  2.14 us

profile of v2, /device:TPU:217, one launch (start us, length us, event | category | flops | bytes accessed | tf_op | source)
XLA Modules:
  0.0 26.1 jit_solution(5319206168776490749)
XLA Ops:
  0.6 23.3 %step.1 = (f32[4,16,256]{2,1,0:T(8,128)}, f32[4,16,256]{2,1,0:T(8,128)}) custom-call(f32[4,16,256]{2,1,0:T(8,128)} %refs_0_.1, f32[4,16,256]{2,1,0:T(8,128)} %refs_1_.1, f32[2,4,16,256]{3,2,1,0:T(8,128)} %refs_2_.1, f32[9,256]{1,0:T(8,128)} %refs_3_.1, s32[4,64]{1,0:T(4,128)} %bitcast.1), custom_call_target="tpu_custom_call" | custom-call | tf_op jit(solution)/shard_map/step/pallas_call | solution.py:505
  23.9 0.0 copy-start
  23.9 1.5 %copy.9 = f32[4,16,256]{2,1,0:T(8,128)} copy(f32[4,16,256]{2,1,0:T(8,128)} %get-tuple-element.4) | data formatting | bytes 131072
  25.5 0.0 copy-done
  25.5 0.6 %copy.10 = f32[4,16,256]{2,1,0:T(8,128)} copy(f32[4,16,256]{2,1,0:T(8,128)S(1)} %copy-done) | data formatting | bytes 131072
Async XLA Ops:
  23.9 1.5 %copy-start = (f32[4,16,256]{2,1,0:T(8,128)S(1)}, f32[4,16,256]{2,1,0:T(8,128)}, u32[]{:S(2)}) copy-start(f32[4,16,256]{2,1,0:T(8,128)} %get-tuple-element.5) | copy-start | bytes 196612

commit v3 on v2

--- a/solution.py
+++ b/solution.py
@@ -66,12 +66,18 @@
     return out, stretch
 
 
+def spread(pair):
+    other = pltpu.roll(pair, 64, 1)
+    left = lax.broadcasted_iota(jnp.int32, pair.shape, 1) < 64
+    return jnp.where(left, pair, other), jnp.where(left, other, pair)
+
+
 def kernel(
     n_x, n_y, split, order,
-    pot_in, rec_in, ang_in, def_in, slot_in, pot_out, rec_out,
-    pot, rec, ang, dfm, slot, ag8, ag1, ysend, yrecv, srecv, xpot, xang, xcor, s8, s1,
-    fib, crs, fine, con, stretch, vh, onew, onev,
-    in_sem, out_sem, ag_send, ag_recv, y_send, y_recv, x_send, x_recv, c_send, c_recv,
+    pot_in, rec_in, ang_in, def_in, slot_in, onev, onew,
+    pot, rec, ang, slot, dfm, ag8, ag1, ysend, yrecv, srecv, beside_x, cc, s8, s1,
+    fib, crs, fine, con, stretch, vh,
+    in_sem, g_send, g_recv, s_send, s_recv, h_send, h_recv, p_send, p_recv, c_send, c_recv,
 ):
     gx = lax.axis_index("gx")
     gy = lax.axis_index("gy")
@@ -95,18 +101,27 @@
     barrier = pltpu.get_barrier_semaphore()
     for number in order:
         pl.semaphore_signal(barrier, inc=1, device_id=(gx, peer(number)), device_id_type=MESH)
-    for there, device, _ in x_sides:
+    count = n_y - 1
+    for there, device, *_ in x_sides:
 
         @pl.when(there)
         def _(device=device):
             pl.semaphore_signal(barrier, inc=1, device_id=device, device_id_type=MESH)
+
+        count += jnp.where(there, 1, 0)
 
     for load in loads[1:]:
         load.start()
     loads[0].wait()
     ag8[0] = dfm[0:8]
     ag1[0] = dfm[8:9]
-    pl.semaphore_wait(barrier, n_y - 1 + jnp.where(first_x, 0, 1) + jnp.where(last_x, 0, 1))
+    for load in loads[1:]:
+        load.wait()
+    for side, (_, _, row) in enumerate(y_sides):
+        ysend[side, 0:4] = pot[:, row, :]
+        ysend[side, 4:8] = ang[0, :, row, :]
+        ysend[side, 8:12] = ang[1, :, row, :]
+    pl.semaphore_wait(barrier, count)
 
     def remote(src, dst, send_sem, recv_sem, device):
         return pltpu.make_async_remote_copy(
@@ -120,77 +135,52 @@
             for copy in copies:
                 copy.start()
 
-    def arrived(there, copies, otherwise):
+    def whole(ref, semaphore):
+        return pltpu.make_async_copy(ref, ref, semaphore)
+
+    def arrived(there, ref, semaphore, otherwise):
         @pl.when(there)
         def _():
-            for copy in copies:
-                copy.wait_recv()
+            whole(ref, semaphore).wait()
 
         @pl.when(jnp.logical_not(there))
         def _():
             otherwise()
 
-    def sent(there, copies):
+    def sent(there, ref, semaphore):
         @pl.when(there)
         def _():
-            for copy in copies:
-                copy.wait_send()
-
-    gathers = []
-    for number in order:
-        device = (gx, peer(number))
-        gathers += [
-            remote(ag8.at[0], ag8.at[number], ag_send.at[0, number], ag_recv.at[0, number], device),
-            remote(ag1.at[0], ag1.at[number], ag_send.at[1, number], ag_recv.at[1, number], device),
-        ]
-        for copy in gathers[-2:]:
-            copy.start()
-    loads[1].wait()
-    loads[2].wait()
-    loads[3].wait()
-    halos, planes, corners, coarse = [], [], [], []
-    for side, (there, device, row) in enumerate(y_sides):
-        ysend[side, 0:4] = pot[:, row, :]
-        ysend[side, 4:8] = ang[0, :, row, :]
-        ysend[side, 8:12] = ang[1, :, row, :]
-        halos.append(
-            [
-                remote(slot, srecv.at[1 - side], y_send.at[0, side], y_recv.at[0, 1 - side], device),
-                remote(ysend.at[side], yrecv.at[1 - side], y_send.at[1, side], y_recv.at[1, 1 - side], device),
-            ]
-        )
-    for side, (there, device, x) in enumerate(x_sides):
+            whole(ref, semaphore).wait()
+
+    gathers = [
+        remote(ref.at[0], ref.at[number], g_send.at[i], g_recv.at[i], (gx, peer(number)))
+        for number in order
+        for i, ref in enumerate((ag8, ag1))
+    ]
+    slots, halos, planes, coarse = [], [], [], []
+    for side, (_, device, _) in enumerate(y_sides):
+        slots.append(remote(slot, srecv.at[1 - side], s_send.at[side], s_recv.at[1 - side], device))
+        halos.append(remote(ysend.at[side], yrecv.at[1 - side], h_send.at[side], h_recv.at[1 - side], device))
+    for side, (_, device, x) in enumerate(x_sides):
         planes.append(
-            [remote(pot.at[x], xpot.at[1 - side], x_send.at[0, side], x_recv.at[0, 1 - side], device)]
-            + [
-                remote(
-                    ang.at[which, x], xang.at[1 - side, which],
-                    x_send.at[1 + which, side], x_recv.at[1 + which, 1 - side], device,
-                )
-                for which in range(2)
-            ]
-        )
-        corners.append(
             [
                 remote(
-                    yrecv.at[which, 0:8], xcor.at[1 - side, which],
-                    x_send.at[3 + which, side], x_recv.at[3 + which, 1 - side], device,
+                    pot.at[x] if i == 0 else ang.at[i - 1, x], beside_x.at[1 - side, i],
+                    p_send.at[side], p_recv.at[1 - side], device,
                 )
-                for which in range(2)
+                for i in range(3)
             ]
         )
-        coarse.append(
-            [
-                remote(s8.at[0], s8.at[2 - side], c_send.at[0, side], c_recv.at[0, 1 - side], device),
-                remote(s1.at[0], s1.at[2 - side], c_send.at[1, side], c_recv.at[1, 1 - side], device),
-            ]
-        )
+        coarse.append(remote(cc.at[0], cc.at[2 - side], c_send.at[side], c_recv.at[1 - side], device))
+    for (there, _, _), copy in zip(y_sides, slots):
+        send(there, [copy])
+    for copy in gathers:
+        copy.start()
+    for (there, _, _), copy in zip(y_sides, halos):
+        send(there, [copy])
     for (there, _, _), copies in zip(x_sides, planes):
         send(there, copies)
-    for (there, _, _), copies in zip(y_sides, halos):
-        send(there, copies)
-
-    loads[4].wait()
+
     for x in range(4):
         v, w = pot[x], rec[x]
         onew[x] = w + time_step * recover_rate * (
@@ -199,35 +189,23 @@
         f = fibers(ang[0, x], ang[1, x])
         for i in range(3):
             fib[i, 16 * (x + 1) : 16 * (x + 2)] = f[i]
-    rec_store = pltpu.make_async_copy(onew, rec_out, out_sem.at[0])
-    rec_store.start()
 
     k_iota = lax.broadcasted_iota(jnp.int32, (128, 256), 0) & 63
     z_iota = lax.broadcasted_iota(jnp.int32, (128, 256), 1)
     place = jnp.clip((z_iota.astype(F32) + 0.5) * 0.25 - 0.5, 0.0, 63.0)
     hat = jnp.maximum(1.0 - jnp.abs(place - k_iota.astype(F32)), 0.0).astype(BF16)
 
-    for side, (there, _, row) in enumerate(y_sides):
-
-        def own_row(side=side, row=row):
-            yrecv[side, 0:12] = ysend[side, 0:12]
+    for side, (there, _, _) in enumerate(y_sides):
+
+        def own_slots(side=side):
             srecv[side] = slot[...]
 
-        arrived(there, halos[1 - side], own_row)
-    for (there, _, _), copies in zip(x_sides, corners):
-        send(there, copies)
-    azimuth = jnp.concatenate([yrecv[0, 4:8], yrecv[1, 4:8]], axis=0)
-    elevation = jnp.concatenate([yrecv[0, 8:12], yrecv[1, 8:12]], axis=0)
-    f = fibers(azimuth, elevation)
-    for i in range(3):
-        fib[i, LAST : LAST + 8] = f[i]
-
+        arrived(there, srecv.at[side], s_recv.at[side], own_slots)
     mine = slot[...]
     below = jnp.where(first_y, mine[0:1], srecv[0, 3:4])
     above = jnp.where(last_y, mine[3:4], srecv[1, 0:1])
     wanted = jnp.concatenate(
-        [piece for row in (below, mine[0:1], mine[1:2], mine[2:3], mine[3:4], above) for piece in (row, row)],
-        axis=1,
+        [below, mine[0:1], mine[1:2], mine[2:3], mine[3:4], above], axis=1
     )
     local = wanted & 255
     holder = (wanted >> 8) & (n_y - 1)
@@ -235,70 +213,78 @@
     from_i = (my_i - (holder & (inner - 1))) & (inner - 1)
     source = from_o * inner + from_i
     hot = jnp.where(
-        lax.broadcasted_iota(jnp.int32, (256, 768), 0) == local, 1.0, 0.0
+        lax.broadcasted_iota(jnp.int32, (256, 384), 0) == local, 1.0, 0.0
     ).astype(BF16)
 
-    for copy in gathers:
-        copy.wait_recv()
-    d8 = ag8[...].reshape(n_y * 8, 256)
-    d1 = ag1[...].reshape(n_y, 256)
-    both = jnp.concatenate([d8, d1], axis=0)
+    whole(ag8.at[1:n_y], g_recv.at[0]).wait()
+    whole(ag1.at[1:n_y], g_recv.at[1]).wait()
+    both = jnp.concatenate([ag8[...].reshape(n_y * 8, 256), ag1[...].reshape(n_y, 256)], axis=0)
     high = both.astype(BF16)
     low = (both - high.astype(F32)).astype(BF16)
     chosen = jnp.dot(high, hot, preferred_element_type=F32) + jnp.dot(
         low, hot, preferred_element_type=F32
     )
-    total = jnp.zeros((8, 768), F32)
+    total = jnp.zeros((8, 384), F32)
     for number in range(n_y):
         total = total + jnp.where(source == number, chosen[8 * number : 8 * number + 8], 0.0)
-    s8[0] = total
     last = chosen[8 * n_y : 9 * n_y]
-    s1[0] = jnp.sum(
-        jnp.where(lax.broadcasted_iota(jnp.int32, (n_y, 768), 0) == source, last, 0.0),
+    cc[0, 0:8] = total
+    cc[0, 8:9] = jnp.sum(
+        jnp.where(lax.broadcasted_iota(jnp.int32, (n_y, 384), 0) == source, last, 0.0),
         axis=0, keepdims=True,
     )
-    for i in range(2):
-        for (there, _, _), copies in zip(x_sides, coarse):
-            send(there, copies[i : i + 1])
-
+
+    for side, (there, _, row) in enumerate(y_sides):
+
+        def own_row(side=side):
+            yrecv[side, 0:12] = ysend[side, 0:12]
+
+        arrived(there, yrecv.at[side], h_recv.at[side], own_row)
     for side, (there, _, x) in enumerate(x_sides):
+        row = 9 + 2 * side
+        for which in range(2):
+            cc[0, row + which : row + which + 1, 0:256] = yrecv[which, x : x + 1]
+    for (there, _, _), copy in zip(x_sides, coarse):
+        send(there, [copy])
+
+    for side, (there, _, x) in enumerate(x_sides):
 
         def own_plane(side=side, x=x):
-            xpot[side] = pot[x]
-            xang[side] = ang[:, x]
-            for which in range(2):
-                for i in (0, 3):
-                    xcor[side, which, i : i + 1] = yrecv[which, x : x + 1]
-
-        arrived(there, planes[1 - side] + corners[1 - side], own_plane)
+            beside_x[side, 0] = pot[x]
+            beside_x[side, 1:3] = ang[:, x]
+
+        arrived(there, beside_x.at[side], p_recv.at[side], own_plane)
+    azimuth = jnp.concatenate([yrecv[0, 4:8], yrecv[1, 4:8]], axis=0)
+    elevation = jnp.concatenate([yrecv[0, 8:12], yrecv[1, 8:12]], axis=0)
+    f = fibers(azimuth, elevation)
+    for i in range(3):
+        fib[i, LAST : LAST + 8] = f[i]
     for side, start in ((0, 0), (1, 80)):
-        f = fibers(xang[side, 0], xang[side, 1])
+        f = fibers(beside_x[side, 1], beside_x[side, 2])
         for i in range(3):
             fib[i, start : start + 16] = f[i]
-    volt = [xpot[0]] + [pot[x] for x in range(4)] + [xpot[1]]
+    volt = [beside_x[0, 0]] + [pot[x] for x in range(4)] + [beside_x[1, 0]]
+    for side, (there, _, _) in enumerate(x_sides):
+
+        def own_elements(side=side):
+            cc[1 + side] = cc[0]
+            for which in range(2):
+                row = 11 - 2 * side + which
+                cc[1 + side, row : row + 1] = cc[0, 9 + 2 * side + which : 10 + 2 * side + which]
+
+        arrived(there, cc.at[1 + side], c_recv.at[side], own_elements)
     for which, row, outside in ((0, 0, first_y), (1, 15, last_y)):
-        ring = [
-            xcor[0, which, 3:4],
-            yrecv[which, 0:1], yrecv[which, 1:2], yrecv[which, 2:3], yrecv[which, 3:4],
-            xcor[1, which, 0:1],
-        ]
+        ring = [cc[1, 11 + which : 12 + which, 0:256]]
+        ring += [yrecv[which, x : x + 1] for x in range(4)]
+        ring += [cc[2, 9 + which : 10 + which, 0:256]]
         for p in range(6):
             vh[which, p : p + 1] = jnp.where(outside, volt[p][row : row + 1], ring[p])
-
-    for copy in gathers:
-        copy.wait_send()
-    for (there, _, _), copies in zip(y_sides, halos):
-        sent(there, copies)
-    for (there, _, _), first, second in zip(x_sides, planes, corners):
-        sent(there, first + second)
-
-    for side, (there, _, _) in enumerate(x_sides):
-
-        def own_elements(side=side):
-            s8[1 + side] = s8[0]
-            s1[1 + side] = s1[0]
-
-        arrived(there, coarse[1 - side], own_elements)
+    for which in range(3):
+        for rows, to in ((slice(0, 8), s8), (slice(8, 9), s1)):
+            for i in range(3):
+                pair = spread(cc[which, rows, 128 * i : 128 * i + 128])
+                for j in range(2):
+                    to[which, :, 128 * (2 * i + j) : 128 * (2 * i + j + 1)] = pair[j]
     sub = lax.broadcasted_iota(jnp.int32, (8, 128), 0)
 
     def hat_rows(start, element):
@@ -437,12 +423,22 @@
             v - stretch_reversal
         )
         onev[x] = v + time_step * (divergent - current)
-    pot_store = pltpu.make_async_copy(onev, pot_out, out_sem.at[1])
-    pot_store.start()
-    for (there, _, _), copies in zip(x_sides, coarse):
-        sent(there, copies)
-    rec_store.wait()
-    pot_store.wait()
+    whole(ag8.at[1:n_y], g_send.at[0]).wait()
+    whole(ag1.at[1:n_y], g_send.at[1]).wait()
+    for side, (there, _, _) in enumerate(y_sides):
+        sent(there, srecv.at[side], s_send.at[side])
+        sent(there, yrecv.at[side], h_send.at[side])
+    for side, (there, _, _) in enumerate(x_sides):
+        sent(there, beside_x.at[side], p_send.at[side])
+        sent(there, cc.at[1 + side], c_send.at[side])
+
+
+def store(pot, rec, pot_out, rec_out, sem):
+    copies = [pltpu.make_async_copy(a, b, sem.at[i]) for i, (a, b) in enumerate(((pot, pot_out), (rec, rec_out)))]
+    for copy in copies:
+        copy.start()
+    for copy in copies:
+        copy.wait()
 
 
 def make_local(n_x, n_y):
@@ -462,22 +458,21 @@
         call = pl.pallas_call(
             lambda *refs: kernel(n_x, n_y, split, order, *refs),
             out_shape=(jax.ShapeDtypeStruct(cells, F32),) * 2,
-            in_specs=[anywhere] * 5,
-            out_specs=(anywhere, anywhere),
+            in_specs=[pl.BlockSpec(memory_space=pltpu.HBM)] * 5,
+            out_specs=(pl.BlockSpec(memory_space=pltpu.VMEM),) * 2,
             scratch_shapes=[
                 pltpu.VMEM(cells, F32),
                 pltpu.VMEM(cells, F32),
                 pltpu.VMEM((2,) + cells, F32),
+                pltpu.VMEM((4, 64), jnp.int32),
                 pltpu.VMEM((9, 256), F32),
-                pltpu.VMEM((4, 64), jnp.int32),
                 pltpu.VMEM((n_y, 8, 256), F32),
                 pltpu.VMEM((n_y, 1, 256), F32),
                 pltpu.VMEM((2, 16, 256), F32),
                 pltpu.VMEM((2, 16, 256), F32),
                 pltpu.VMEM((2, 4, 64), jnp.int32),
-                pltpu.VMEM((2, 16, 256), F32),
-                pltpu.VMEM((2, 2, 16, 256), F32),
-                pltpu.VMEM((2, 2, 8, 256), F32),
+                pltpu.VMEM((2, 3, 16, 256), F32),
+                pltpu.VMEM((3, 16, 384), F32),
                 pltpu.VMEM((3, 8, 768), F32),
                 pltpu.VMEM((3, 1, 768), F32),
                 pltpu.VMEM((3, ROWS, 256), F32),
@@ -486,23 +481,34 @@
                 pltpu.VMEM((6, ROWS, 256), F32),
                 pltpu.VMEM((64, 256), F32),
                 pltpu.VMEM((2, 8, 256), F32),
-                pltpu.VMEM(cells, F32),
-                pltpu.VMEM(cells, F32),
                 dma((5,)),
                 dma((2,)),
-                dma((2, n_y)),
-                dma((2, n_y)),
-                dma((2, 2)),
-                dma((2, 2)),
-                dma((5, 2)),
-                dma((5, 2)),
-                dma((2, 2)),
-                dma((2, 2)),
+                dma((2,)),
+                dma((2,)),
+                dma((2,)),
+                dma((2,)),
+                dma((2,)),
+                dma((2,)),
+                dma((2,)),
+                dma((2,)),
+                dma((2,)),
             ],
-            compiler_params=pltpu.CompilerParams(collective_id=0, has_side_effects=True),
+            compiler_params=pltpu.CompilerParams(
+                collective_id=0, has_side_effects=True, vmem_limit_bytes=16 * 2**20
+            ),
             name="step",
         )
-        return call(potential, recovery, fiber_angles, deform, elem_slot.reshape(4, 64))
+        args = (potential, recovery, fiber_angles, deform, elem_slot.reshape(4, 64))
+        held = call(*(pltpu.with_memory_space_constraint(a, pltpu.HBM) for a in args))
+        return pl.pallas_call(
+            store,
+            out_shape=(jax.ShapeDtypeStruct(cells, F32),) * 2,
+            in_specs=[pl.BlockSpec(memory_space=pltpu.VMEM)] * 2,
+            out_specs=(anywhere, anywhere),
+            scratch_shapes=[dma((2,))],
+            compiler_params=pltpu.CompilerParams(vmem_limit_bytes=16 * 2**20),
+            name="store",
+        )(*held)
 
     return local
 

time: 26.3 us -> 22.8 us (0.87)
  the two profiles are of different devices: /device:TPU:217 before, /device:TPU:201 now
where the time goes in v3:
time: 22.8 us; the launch traced here: 22.6 us
  Pallas kernels  22 us (96%)
  between operations  0.64 us (3%)
    pallas_call x1, Pallas kernels, local(): call(*(pltpu.with_memory_space_constraint(a, pltpu.HBM) for a in args))  21.3 us
    pallas_call x1, Pallas kernels, local(): pl.pallas_call(store, out_shape=(jax.ShapeDtypeStruct(cells, F32),) * 2,...  0.67 us

profile of v3, /device:TPU:201, one launch (start us, length us, event | category | flops | bytes accessed | tf_op | source)
XLA Modules:
  0.0 22.6 jit_solution(4185742581313493964)
XLA Ops:
  0.6 21.3 %step.1 = (f32[4,16,256]{2,1,0:T(8,128)S(1)}, f32[4,16,256]{2,1,0:T(8,128)S(1)}) custom-call(f32[4,16,256]{2,1,0:T(8,128)} %refs_0_.1, f32[4,16,256]{2,1,0:T(8,128)} %refs_1_.1, f32[2,4,16,256]{3,2,1,0:T(8,128)} %refs_2_.1, f32[9,256]{1,0:T(8,128)} %refs_3_.1, s32[4,64]{1,0:T(4,128)} %bitcast.1), custom_call_target="tpu_custom_call" | custom-call | tf_op jit(solution)/shard_map/step/pallas_call | solution.py:502
  21.9 0.7 %store.1 = (f32[4,16,256]{2,1,0:T(8,128)}, f32[4,16,256]{2,1,0:T(8,128)}) custom-call(f32[4,16,256]{2,1,0:T(8,128)S(1)} %get-tuple-element.4.pot, f32[4,16,256]{2,1,0:T(8,128)S(1)} %get-tuple-element.5.rec), custom_call_target="tpu_custom_call" | custom-call | tf_op jit(solution)/shard_map/store/pallas_call | solution.py:503

commit v4 on v3

--- a/solution.py
+++ b/solution.py
@@ -18,8 +18,16 @@
 F32 = jnp.float32
 BF16 = jnp.bfloat16
 
-ROWS = 104
-LAST = 96
+HALF = 56
+ROWS = 112
+
+
+def plane_row(p):
+    return 16 * p if p < 3 else HALF + 16 * (p - 3)
+
+
+def beside_row(x, which):
+    return 48 + HALF * (x // 2) + 2 * which + x % 2
 
 
 def sin_cos(angle):
@@ -76,7 +84,7 @@
     n_x, n_y, split, order,
     pot_in, rec_in, ang_in, def_in, slot_in, onev, onew,
     pot, rec, ang, slot, dfm, ag8, ag1, ysend, yrecv, srecv, beside_x, cc, s8, s1,
-    fib, crs, fine, con, stretch, vh,
+    fib, mid, crs, fine, con, stretch, vh,
     in_sem, g_send, g_recv, s_send, s_recv, h_send, h_recv, p_send, p_recv, c_send, c_recv,
 ):
     gx = lax.axis_index("gx")
@@ -188,7 +196,7 @@
         )
         f = fibers(ang[0, x], ang[1, x])
         for i in range(3):
-            fib[i, 16 * (x + 1) : 16 * (x + 2)] = f[i]
+            fib[i, plane_row(x + 1) : plane_row(x + 1) + 16] = f[i]
 
     k_iota = lax.broadcasted_iota(jnp.int32, (128, 256), 0) & 63
     z_iota = lax.broadcasted_iota(jnp.int32, (128, 256), 1)
@@ -247,102 +255,48 @@
     for (there, _, _), copy in zip(x_sides, coarse):
         send(there, [copy])
 
-    for side, (there, _, x) in enumerate(x_sides):
-
-        def own_plane(side=side, x=x):
-            beside_x[side, 0] = pot[x]
-            beside_x[side, 1:3] = ang[:, x]
-
-        arrived(there, beside_x.at[side], p_recv.at[side], own_plane)
-    azimuth = jnp.concatenate([yrecv[0, 4:8], yrecv[1, 4:8]], axis=0)
-    elevation = jnp.concatenate([yrecv[0, 8:12], yrecv[1, 8:12]], axis=0)
-    f = fibers(azimuth, elevation)
-    for i in range(3):
-        fib[i, LAST : LAST + 8] = f[i]
-    for side, start in ((0, 0), (1, 80)):
-        f = fibers(beside_x[side, 1], beside_x[side, 2])
-        for i in range(3):
-            fib[i, start : start + 16] = f[i]
-    volt = [beside_x[0, 0]] + [pot[x] for x in range(4)] + [beside_x[1, 0]]
-    for side, (there, _, _) in enumerate(x_sides):
-
-        def own_elements(side=side):
-            cc[1 + side] = cc[0]
-            for which in range(2):
-                row = 11 - 2 * side + which
-                cc[1 + side, row : row + 1] = cc[0, 9 + 2 * side + which : 10 + 2 * side + which]
-
-        arrived(there, cc.at[1 + side], c_recv.at[side], own_elements)
-    for which, row, outside in ((0, 0, first_y), (1, 15, last_y)):
-        ring = [cc[1, 11 + which : 12 + which, 0:256]]
-        ring += [yrecv[which, x : x + 1] for x in range(4)]
-        ring += [cc[2, 9 + which : 10 + which, 0:256]]
-        for p in range(6):
-            vh[which, p : p + 1] = jnp.where(outside, volt[p][row : row + 1], ring[p])
-    for which in range(3):
+    def onto_lanes(which):
         for rows, to in ((slice(0, 8), s8), (slice(8, 9), s1)):
             for i in range(3):
                 pair = spread(cc[which, rows, 128 * i : 128 * i + 128])
                 for j in range(2):
                     to[which, :, 128 * (2 * i + j) : 128 * (2 * i + j + 1)] = pair[j]
+
     sub = lax.broadcasted_iota(jnp.int32, (8, 128), 0)
 
-    def hat_rows(start, element):
-        t = (sub.astype(F32) + (start + 0.5)) * 0.25 - 0.5
+    def hat_rows(at, element):
+        t = at.astype(F32) * 0.25 + (0.125 - 0.5)
         return jnp.maximum(1.0 - jnp.abs(t - element), 0.0)
 
-    tile0 = [hat_rows(0, e - 1) for e in range(4)]
-    tile1 = [hat_rows(8, e + 1) for e in range(4)]
-    t = ((sub & 3).astype(F32) + 0.5) * 0.25 - 0.5
-    cross = [jnp.maximum(1.0 - jnp.abs(t - (e - 1)), 0.0) for e in range(3)]
-    low_half = sub < 4
+    tile0 = [hat_rows(sub, e - 1) for e in range(4)]
+    tile1 = [hat_rows(sub + 8, e + 1) for e in range(4)]
+
+    def along_y(which, k):
+        rows = []
+        for e in range(6):
+            lanes = slice(128 * e, 128 * e + 128)
+            row = s8[which, k : k + 1, lanes] if k < 8 else s1[which, :, lanes]
+            rows.append(jnp.broadcast_to(row, (8, 128)))
+        return (
+            sum(tile0[i] * rows[i] for i in range(4)),
+            sum(tile1[i] * rows[i + 2] for i in range(4)),
+            jnp.where(
+                (sub & 2) == 0, 0.625 * rows[0] + 0.375 * rows[1], 0.625 * rows[5] + 0.375 * rows[4]
+            ),
+        )
+
+    onto_lanes(0)
     for k in range(9):
-        tiles0, tiles1, beside = [], [], []
-        for which in (1, 0, 2):
-            rows = []
-            for e in range(6):
-                lanes = slice(128 * e, 128 * e + 128)
-                row = s8[which, k : k + 1, lanes] if k < 8 else s1[which, :, lanes]
-                rows.append(jnp.broadcast_to(row, (8, 128)))
-            tiles0.append(sum(tile0[i] * rows[i] for i in range(4)))
-            tiles1.append(sum(tile1[i] * rows[i + 2] for i in range(4)))
-            beside.append(
-                jnp.where(low_half, 0.625 * rows[0] + 0.375 * rows[1], 0.625 * rows[5] + 0.375 * rows[4])
-            )
-        base = ROWS * k
-        for p, (a, b, c) in enumerate(
-            (
-                (0.625, 0.375, 0.0), (0.375, 0.625, 0.0), (0.125, 0.875, 0.0),
-                (0.0, 0.875, 0.125), (0.0, 0.625, 0.375), (0.0, 0.375, 0.625),
-            )
-        ):
-            for half, tiles in ((0, tiles0), (8, tiles1)):
-                if c == 0.0:
-                    value = a * tiles[0] + b * tiles[1]
-                else:
-                    value = b * tiles[1] + c * tiles[2]
-                crs[base + 16 * p + half : base + 16 * p + half + 8] = value
-        crs[base + LAST : base + LAST + 8] = (
-            cross[0] * beside[0] + cross[1] * beside[1] + cross[2] * beside[2]
-        )
-    c = crs[...]
-    rest = c - c.astype(BF16).astype(F32)
-    left = lax.broadcasted_iota(jnp.int32, c.shape, 1) < 64
-    fine[...] = jnp.dot(
-        jnp.where(left, c, rest).astype(BF16), hat, preferred_element_type=F32
-    )
-
-    for tile in range(13):
-        at = 8 * tile
-        f = [fine[ROWS * k + at : ROWS * k + at + 8] for k in range(9)]
-        fiber = [fib[i, at : at + 8] for i in range(3)]
-        own = 2 <= tile < 10
-        d, s = tensor_rows(f, fiber, own)
-        for i in range(6):
-            con[i, at : at + 8] = d[i]
-        if own:
-            stretch[at - 16 : at - 8] = s
-
+        for i, value in enumerate(along_y(0, k)):
+            mid[k, i] = value
+    for half in range(2):
+        crs[half, 9 * HALF :] = jnp.zeros((8, 128), F32)
+        rows = [yrecv[which, at + 2 * half : at + 2 * half + 2] for at in (4, 8) for which in range(2)]
+        f = fibers(
+            jnp.concatenate([rows[0], rows[1]] * 2, axis=0), jnp.concatenate([rows[2], rows[3]] * 2, axis=0)
+        )
+        for i in range(3):
+            fib[i, HALF * half + 48 : HALF * half + 56] = f[i]
     row_iota = lax.broadcasted_iota(jnp.int32, (16, 256), 0)
     lane = lax.broadcasted_iota(jnp.int32, (16, 256), 1)
 
@@ -352,9 +306,11 @@
     def from_above(a, edge):
         return jnp.where(row_iota == 15, edge, pltpu.roll(a, 15, 0))
 
+    def onward(a):
+        return pltpu.roll(a, 255, 1)
+
     def z_slope(v):
-        n = v.shape[0]
-        at = lax.broadcasted_iota(jnp.int32, (n, 256), 1)
+        at = lax.broadcasted_iota(jnp.int32, v.shape, 1)
         after = jnp.where(at == 255, v, pltpu.roll(v, 255, 1))
         before = jnp.where(at == 0, v, pltpu.roll(v, 1, 1))
         return after - before
@@ -363,66 +319,129 @@
         return 0.5 * (d1 * step + 0.25 * (d2 * s2 + d3 * s3))
 
     XX, YY, ZZ, XY, XZ, YZ = range(6)
-    slope_y = [from_above(volt[p], vh[1, p : p + 1]) - from_below(volt[p], vh[0, p : p + 1]) for p in range(6)]
-    slope_z = [z_slope(volt[p]) for p in range(6)]
-    edge_z = [z_slope(vh[which]) for which in range(2)]
 
     def plane(i, p):
-        return con[i, 16 * p : 16 * p + 16]
-
-    flux_x = []
-    for p in range(5):
-        value = flux(
-            plane(XX, p) + plane(XX, p + 1), volt[p + 1] - volt[p],
-            plane(XY, p) + plane(XY, p + 1), slope_y[p] + slope_y[p + 1],
-            plane(XZ, p) + plane(XZ, p + 1), slope_z[p] + slope_z[p + 1],
-        )
-        if p == 0:
-            value = jnp.where(first_x, 0.0, value)
-        if p == 4:
-            value = jnp.where(last_x, 0.0, value)
-        flux_x.append(value)
-    for x in range(4):
-        p = x + 1
-        v = volt[p]
-        slope_x = volt[p + 1] - volt[p - 1]
-        d_xy, d_yy, d_yz = plane(XY, p), plane(YY, p), plane(YZ, p)
-        faces = []
-        for which, shift in ((0, from_below), (1, from_above)):
-            row = LAST + 4 * which + x
-            step = shift(v, vh[which, p : p + 1])
-            step = v - step if which == 0 else step - v
-            faces.append(
-                flux(
-                    d_yy + shift(d_yy, con[YY, row : row + 1]), step,
-                    d_xy + shift(d_xy, con[XY, row : row + 1]),
-                    slope_x + shift(slope_x, vh[which, p + 1 : p + 2] - vh[which, p - 1 : p]),
-                    d_yz + shift(d_yz, con[YZ, row : row + 1]),
-                    slope_z[p] + shift(slope_z[p], edge_z[which][p : p + 1]),
+        return con[i, plane_row(p) : plane_row(p) + 16]
+
+    ends = ((0, 0, first_y), (1, 15, last_y))
+    for which, row, outside in ends:
+        vh[which] = jnp.zeros((8, 256), F32)
+        for x in range(4):
+            vh[which, x + 1 : x + 2] = jnp.where(outside, pot[x, row : row + 1], yrecv[which, x : x + 1])
+
+    slope_y, slope_z = [None] * 6, [None] * 6
+    between = None
+    for half, (there, _, x) in enumerate(x_sides):
+
+        def own_plane(half=half, x=x):
+            beside_x[half, 0] = pot[x]
+            beside_x[half, 1:3] = ang[:, x]
+
+        def own_elements(half=half):
+            cc[1 + half] = cc[0]
+            for which in range(2):
+                row = 11 - 2 * half + which
+                cc[1 + half, row : row + 1] = cc[0, 9 + 2 * half + which : 10 + 2 * half + which]
+
+        arrived(there, beside_x.at[half], p_recv.at[half], own_plane)
+        f = fibers(beside_x[half, 1], beside_x[half, 2])
+        outer_p = 5 * half
+        for i in range(3):
+            fib[i, plane_row(outer_p) : plane_row(outer_p) + 16] = f[i]
+        arrived(there, cc.at[1 + half], c_recv.at[half], own_elements)
+
+        onto_lanes(1 + half)
+        t = hat_rows((sub & 1) + 2 * half, 0), hat_rows((sub & 1) + 2 * half, 2 * half - 1)
+        weights = ((0.625, 0.375), (0.375, 0.625), (0.125, 0.875))
+        for k in range(9):
+            side = along_y(1 + half, k)
+            base = HALF * k
+            for number, (a, b) in enumerate(weights[:: 1 - 2 * half]):
+                for i in range(2):
+                    at = base + 16 * number + 8 * i
+                    crs[half, at : at + 8] = a * side[i] + b * mid[k, i]
+            crs[half, base + 48 : base + 56] = t[0] * mid[k, 2] + t[1] * side[2]
+        c = crs[half]
+        rest = c - c.astype(BF16).astype(F32)
+        left = lax.broadcasted_iota(jnp.int32, c.shape, 1) < 64
+        fine[half] = jnp.dot(
+            jnp.where(left, c, rest).astype(BF16), hat, preferred_element_type=F32
+        )
+        for tile in range(7):
+            at = 8 * tile
+            row = HALF * half + at
+            f = [fine[half, HALF * k + at : HALF * k + at + 8] for k in range(9)]
+            fiber = [fib[i, row : row + 8] for i in range(3)]
+            inside = (2 <= tile < 6) if half == 0 else tile < 4
+            d, length = tensor_rows(f, fiber, inside)
+            for i in range(6):
+                con[i, row : row + 8] = d[i]
+            if inside:
+                stretch[row : row + 8] = length
+
+        for which, row, outside in ends:
+            corner = cc[1 + half, 11 - 2 * half + which : 12 - 2 * half + which, 0:256]
+            vh[which, outer_p : outer_p + 1] = jnp.where(outside, beside_x[half, 0, row : row + 1], corner)
+        volt = [beside_x[0, 0]] + [pot[x] for x in range(4)] + [beside_x[1, 0]]
+        edge_z = [z_slope(vh[which]) for which in range(2)]
+        for p in range(3 * half, 3 * half + 3):
+            slope_y[p] = from_above(volt[p], vh[1, p : p + 1]) - from_below(volt[p], vh[0, p : p + 1])
+            slope_z[p] = z_slope(volt[p])
+
+        def across(p):
+            return flux(
+                plane(XX, p) + plane(XX, p + 1), volt[p + 1] - volt[p],
+                plane(XY, p) + plane(XY, p + 1), slope_y[p] + slope_y[p + 1],
+                plane(XZ, p) + plane(XZ, p + 1), slope_z[p] + slope_z[p + 1],
+            )
+
+        def within(x):
+            p = x + 1
+            v = volt[p]
+            slope_x = volt[p + 1] - volt[p - 1]
+            d_xy, d_yy, d_yz = plane(XY, p), plane(YY, p), plane(YZ, p)
+            faces = []
+            for which, shift in ((0, from_below), (1, from_above)):
+                row = beside_row(x, which)
+                step = shift(v, vh[which, p : p + 1])
+                step = v - step if which == 0 else step - v
+                faces.append(
+                    flux(
+                        d_yy + shift(d_yy, con[YY, row : row + 1]), step,
+                        d_xy + shift(d_xy, con[XY, row : row + 1]),
+                        slope_x + shift(slope_x, vh[which, p + 1 : p + 2] - vh[which, p - 1 : p]),
+                        d_yz + shift(d_yz, con[YZ, row : row + 1]),
+                        slope_z[p] + shift(slope_z[p], edge_z[which][p : p + 1]),
+                    )
                 )
+            faces[0] = jnp.where((row_iota == 0) & first_y, 0.0, faces[0])
+            faces[1] = jnp.where((row_iota == 15) & last_y, 0.0, faces[1])
+            d_xz, d_zz = plane(XZ, p), plane(ZZ, p)
+            upper = flux(
+                d_zz + onward(d_zz), onward(v) - v,
+                d_xz + onward(d_xz), slope_x + onward(slope_x),
+                d_yz + onward(d_yz), slope_y[p] + onward(slope_y[p]),
             )
-        faces[0] = jnp.where((row_iota == 0) & first_y, 0.0, faces[0])
-        faces[1] = jnp.where((row_iota == 15) & last_y, 0.0, faces[1])
-
-        def onward(a):
-            return pltpu.roll(a, 255, 1)
-
-        d_xz, d_zz = plane(XZ, p), plane(ZZ, p)
-        upper = flux(
-            d_zz + onward(d_zz), onward(v) - v,
-            d_xz + onward(d_xz), slope_x + onward(slope_x),
-            d_yz + onward(d_yz), slope_y[p] + onward(slope_y[p]),
-        )
-        upper = jnp.where(lane == 255, 0.0, upper)
-        divergent = (
-            flux_x[p] - flux_x[p - 1] + (faces[1] - faces[0]) + (upper - pltpu.roll(upper, 1, 1))
-        )
-        w = rec[x]
-        current = excite_gain * v * (v - excite_level) * (v - 1.0) + v * w
-        current = current + stretch_gain * jnp.maximum(stretch[16 * x : 16 * x + 16] - 1.0, 0.0) * (
-            v - stretch_reversal
-        )
-        onev[x] = v + time_step * (divergent - current)
+            upper = jnp.where(lane == 255, 0.0, upper)
+            w = rec[x]
+            current = excite_gain * v * (v - excite_level) * (v - 1.0) + v * w
+            long = jnp.maximum(stretch[plane_row(p) : plane_row(p) + 16] - 1.0, 0.0)
+            current = current + stretch_gain * long * (v - stretch_reversal)
+            divergent = (faces[1] - faces[0]) + (upper - pltpu.roll(upper, 1, 1))
+            return v + time_step * (divergent - current)
+
+        if half == 0:
+            below = jnp.where(first_x, 0.0, across(0))
+            middle = across(1)
+            onev[0] = within(0) + time_step * (middle - below)
+            onev[1] = within(1) - time_step * middle
+        else:
+            middle = across(2)
+            upper_face = across(3)
+            last_face = jnp.where(last_x, 0.0, across(4))
+            onev[1] = onev[1] + time_step * middle
+            onev[2] = within(2) + time_step * (upper_face - middle)
+            onev[3] = within(3) + time_step * (last_face - upper_face)
     whole(ag8.at[1:n_y], g_send.at[0]).wait()
     whole(ag1.at[1:n_y], g_send.at[1]).wait()
     for side, (there, _, _) in enumerate(y_sides):
@@ -476,10 +495,11 @@
                 pltpu.VMEM((3, 8, 768), F32),
                 pltpu.VMEM((3, 1, 768), F32),
                 pltpu.VMEM((3, ROWS, 256), F32),
-                pltpu.VMEM((9 * ROWS, 128), F32),
-                pltpu.VMEM((9 * ROWS, 256), F32),
+                pltpu.VMEM((9, 3, 8, 128), F32),
+                pltpu.VMEM((2, 9 * HALF + 8, 128), F32),
+                pltpu.VMEM((2, 9 * HALF + 8, 256), F32),
                 pltpu.VMEM((6, ROWS, 256), F32),
-                pltpu.VMEM((64, 256), F32),
+                pltpu.VMEM((ROWS, 256), F32),
                 pltpu.VMEM((2, 8, 256), F32),
                 dma((5,)),
                 dma((2,)),

time: 22.8 us -> 22.4 us (0.982)
  Pallas kernels: 22 us -> 21.6 us
    pallas_call x1, Pallas kernels: 21.3 us -> 20.9 us  [local(): call(*(pltpu.with_memory_space_constraint(a, pltpu.HBM) for a in args))]
where the time goes in v4:
time: 22.4 us; the launch traced here: 22.2 us
  Pallas kernels  21.6 us (96%)
  between operations  0.64 us (3%)
    pallas_call x1, Pallas kernels, local(): call(*(pltpu.with_memory_space_constraint(a, pltpu.HBM) for a in args))  20.9 us
    pallas_call x1, Pallas kernels, local(): pl.pallas_call(store, out_shape=(jax.ShapeDtypeStruct(cells, F32),) * 2,...  0.67 us

profile of v4, /device:TPU:201, one launch (start us, length us, event | category | flops | bytes accessed | tf_op | source)
XLA Modules:
  0.0 22.2 jit_solution(10128944664706552643)
XLA Ops:
  0.6 20.9 %step.1 = (f32[4,16,256]{2,1,0:T(8,128)S(1)}, f32[4,16,256]{2,1,0:T(8,128)S(1)}) custom-call(f32[4,16,256]{2,1,0:T(8,128)} %refs_0_.1, f32[4,16,256]{2,1,0:T(8,128)} %refs_1_.1, f32[2,4,16,256]{3,2,1,0:T(8,128)} %refs_2_.1, f32[9,256]{1,0:T(8,128)} %refs_3_.1, s32[4,64]{1,0:T(4,128)} %bitcast.1), custom_call_target="tpu_custom_call" | custom-call | tf_op jit(solution)/shard_map/step/pallas_call | solution.py:522
  21.6 0.7 %store.1 = (f32[4,16,256]{2,1,0:T(8,128)}, f32[4,16,256]{2,1,0:T(8,128)}) custom-call(f32[4,16,256]{2,1,0:T(8,128)S(1)} %get-tuple-element.4.pot, f32[4,16,256]{2,1,0:T(8,128)S(1)} %get-tuple-element.5.rec), custom_call_target="tpu_custom_call" | custom-call | tf_op jit(solution)/shard_map/store/pallas_call | solution.py:523

commit v5 on v4

--- a/solution.py
+++ b/solution.py
@@ -74,6 +74,12 @@
     return out, stretch
 
 
+STRAIGHT = ((1, 0), (2, 0), (3, 0), (1, 1), (1, 3), (3, 1), (3, 3))
+COLUMN = ((0, 1), (0, 3), (0, 2))
+RELAYED = ((2, 1), (2, 3), (1, 2), (2, 2), (3, 2))
+PLACES = ((0, 0),) + STRAIGHT + COLUMN + RELAYED
+
+
 def spread(pair):
     other = pltpu.roll(pair, 64, 1)
     left = lax.broadcasted_iota(jnp.int32, pair.shape, 1) < 64
@@ -81,7 +87,7 @@
 
 
 def kernel(
-    n_x, n_y, split, order,
+    n_x, n_y,
     pot_in, rec_in, ang_in, def_in, slot_in, onev, onew,
     pot, rec, ang, slot, dfm, ag8, ag1, ysend, yrecv, srecv, beside_x, cc, s8, s1,
     fib, mid, crs, fine, con, stretch, vh,
@@ -92,12 +98,17 @@
     first_x, last_x, first_y, last_y = gx == 0, gx == n_x - 1, gy == 0, gy == n_y - 1
     x_sides = ((jnp.logical_not(first_x), (gx - 1, gy), 0), (jnp.logical_not(last_x), (gx + 1, gy), 3))
     y_sides = ((jnp.logical_not(first_y), (gx, gy - 1), 0), (jnp.logical_not(last_y), (gx, gy + 1), 15))
-    outer, inner = split
-    my_o, my_i = lax.div(gy, inner), lax.rem(gy, inner)
-
-    def peer(number):
-        step_o, step_i = number // inner, number % inner
-        return lax.rem(my_o + step_o, outer) * inner + lax.rem(my_i + step_i, inner)
+    my_o, my_i = lax.div(gy, 4), lax.rem(gy, 4)
+
+    def peer(o, i):
+        return (gx, lax.rem(my_o + o, 4) * 4 + lax.rem(my_i + i, 4))
+
+    direct = ((0, 2), (0, 1), (0, 3), (1, 1), (1, 3), (3, 1), (3, 3), (2, 0), (1, 0), (3, 0))
+    every = (
+        (2, 2), (1, 2), (3, 2), (0, 2), (2, 1), (2, 3), (1, 1), (1, 3), (3, 1), (3, 3),
+        (0, 1), (0, 3), (2, 0), (1, 0), (3, 0),
+    )
+    late = lax.rem(gx, 2) == 0
 
     loads = [
         pltpu.make_async_copy(src, dst, in_sem.at[i])
@@ -107,9 +118,15 @@
     ]
     loads[0].start()
     barrier = pltpu.get_barrier_semaphore()
-    for number in order:
-        pl.semaphore_signal(barrier, inc=1, device_id=(gx, peer(number)), device_id_type=MESH)
-    count = n_y - 1
+    for steps in direct:
+        pl.semaphore_signal(barrier, inc=1, device_id=peer(*steps), device_id_type=MESH)
+
+    @pl.when(late)
+    def _():
+        for steps in RELAYED:
+            pl.semaphore_signal(barrier, inc=1, device_id=peer(*steps), device_id_type=MESH)
+
+    count = len(direct) + jnp.where(late, len(RELAYED), 0)
     for there, device, *_ in x_sides:
 
         @pl.when(there)
@@ -160,11 +177,29 @@
         def _():
             whole(ref, semaphore).wait()
 
-    gathers = [
-        remote(ref.at[0], ref.at[number], g_send.at[i], g_recv.at[i], (gx, peer(number)))
-        for number in order
-        for i, ref in enumerate((ag8, ag1))
-    ]
+    def piece(place, steps, device, group):
+        return [
+            remote(ref.at[place], ref.at[PLACES.index(steps)], g_send.at[k], g_recv.at[group, k], device)
+            for k, ref in enumerate((ag8, ag1))
+        ]
+
+    def gather(steps):
+        group = 1 + COLUMN.index(steps) if steps in COLUMN else 4 if steps in RELAYED else 0
+        for copy in piece(0, steps, peer(*steps), group):
+            copy.start()
+
+    def relay(steps):
+        at, group = PLACES.index(steps), 1 + COLUMN.index(steps)
+        for k, ref in enumerate((ag8, ag1)):
+            whole(ref.at[at], g_recv.at[group, k]).wait()
+
+        @pl.when(jnp.logical_not(late))
+        def _():
+            for o in (2, 1, 3):
+                to = (o, steps[1])
+                for copy in piece(at, to, peer(o, 0), 4 if to in RELAYED else 0):
+                    copy.start()
+
     slots, halos, planes, coarse = [], [], [], []
     for side, (_, device, _) in enumerate(y_sides):
         slots.append(remote(slot, srecv.at[1 - side], s_send.at[side], s_recv.at[1 - side], device))
@@ -182,8 +217,18 @@
         coarse.append(remote(cc.at[0], cc.at[2 - side], c_send.at[side], c_recv.at[1 - side], device))
     for (there, _, _), copy in zip(y_sides, slots):
         send(there, [copy])
-    for copy in gathers:
-        copy.start()
+
+    @pl.when(late)
+    def _():
+        for steps in every:
+            gather(steps)
+
+    @pl.when(jnp.logical_not(late))
+    def _():
+        for steps in direct:
+            if 0 in steps:
+                gather(steps)
+
     for (there, _, _), copy in zip(y_sides, halos):
         send(there, [copy])
     for (there, _, _), copies in zip(x_sides, planes):
@@ -202,6 +247,9 @@
     z_iota = lax.broadcasted_iota(jnp.int32, (128, 256), 1)
     place = jnp.clip((z_iota.astype(F32) + 0.5) * 0.25 - 0.5, 0.0, 63.0)
     hat = jnp.maximum(1.0 - jnp.abs(place - k_iota.astype(F32)), 0.0).astype(BF16)
+
+    relay((0, 1))
+    relay((0, 3))
 
     for side, (there, _, _) in enumerate(y_sides):
 
@@ -216,16 +264,18 @@
         [below, mine[0:1], mine[1:2], mine[2:3], mine[3:4], above], axis=1
     )
     local = wanted & 255
-    holder = (wanted >> 8) & (n_y - 1)
-    from_o = (my_o - (holder >> (inner.bit_length() - 1))) & (outer - 1)
-    from_i = (my_i - (holder & (inner - 1))) & (inner - 1)
-    source = from_o * inner + from_i
+    source = (((my_o - (wanted >> 10)) & 3) << 2) | ((my_i - (wanted >> 8)) & 3)
+    place_iota = lax.broadcasted_iota(jnp.int32, (n_y, 384), 0)
+    place_source = sum(jnp.where(place_iota == at, 4 * o + i, 0) for at, (o, i) in enumerate(PLACES))
     hot = jnp.where(
         lax.broadcasted_iota(jnp.int32, (256, 384), 0) == local, 1.0, 0.0
     ).astype(BF16)
 
-    whole(ag8.at[1:n_y], g_recv.at[0]).wait()
-    whole(ag1.at[1:n_y], g_recv.at[1]).wait()
+    relay((0, 2))
+
+    for k, ref in enumerate((ag8, ag1)):
+        whole(ref.at[1:8], g_recv.at[0, k]).wait()
+        whole(ref.at[11:16], g_recv.at[4, k]).wait()
     both = jnp.concatenate([ag8[...].reshape(n_y * 8, 256), ag1[...].reshape(n_y, 256)], axis=0)
     high = both.astype(BF16)
     low = (both - high.astype(F32)).astype(BF16)
@@ -233,12 +283,12 @@
         low, hot, preferred_element_type=F32
     )
     total = jnp.zeros((8, 384), F32)
-    for number in range(n_y):
-        total = total + jnp.where(source == number, chosen[8 * number : 8 * number + 8], 0.0)
+    for at, (o, i) in enumerate(PLACES):
+        total = total + jnp.where(source == 4 * o + i, chosen[8 * at : 8 * at + 8], 0.0)
     last = chosen[8 * n_y : 9 * n_y]
     cc[0, 0:8] = total
     cc[0, 8:9] = jnp.sum(
-        jnp.where(lax.broadcasted_iota(jnp.int32, (n_y, 384), 0) == source, last, 0.0),
+        jnp.where(place_source == source, last, 0.0),
         axis=0, keepdims=True,
     )
 
@@ -329,119 +379,131 @@
         for x in range(4):
             vh[which, x + 1 : x + 2] = jnp.where(outside, pot[x, row : row + 1], yrecv[which, x : x + 1])
 
-    slope_y, slope_z = [None] * 6, [None] * 6
-    between = None
-    for half, (there, _, x) in enumerate(x_sides):
-
-        def own_plane(half=half, x=x):
-            beside_x[half, 0] = pot[x]
-            beside_x[half, 1:3] = ang[:, x]
-
-        def own_elements(half=half):
-            cc[1 + half] = cc[0]
-            for which in range(2):
-                row = 11 - 2 * half + which
-                cc[1 + half, row : row + 1] = cc[0, 9 + 2 * half + which : 10 + 2 * half + which]
-
-        arrived(there, beside_x.at[half], p_recv.at[half], own_plane)
-        f = fibers(beside_x[half, 1], beside_x[half, 2])
-        outer_p = 5 * half
-        for i in range(3):
-            fib[i, plane_row(outer_p) : plane_row(outer_p) + 16] = f[i]
-        arrived(there, cc.at[1 + half], c_recv.at[half], own_elements)
-
-        onto_lanes(1 + half)
-        t = hat_rows((sub & 1) + 2 * half, 0), hat_rows((sub & 1) + 2 * half, 2 * half - 1)
-        weights = ((0.625, 0.375), (0.375, 0.625), (0.125, 0.875))
-        for k in range(9):
-            side = along_y(1 + half, k)
-            base = HALF * k
-            for number, (a, b) in enumerate(weights[:: 1 - 2 * half]):
-                for i in range(2):
-                    at = base + 16 * number + 8 * i
-                    crs[half, at : at + 8] = a * side[i] + b * mid[k, i]
-            crs[half, base + 48 : base + 56] = t[0] * mid[k, 2] + t[1] * side[2]
-        c = crs[half]
-        rest = c - c.astype(BF16).astype(F32)
-        left = lax.broadcasted_iota(jnp.int32, c.shape, 1) < 64
-        fine[half] = jnp.dot(
-            jnp.where(left, c, rest).astype(BF16), hat, preferred_element_type=F32
-        )
-        for tile in range(7):
-            at = 8 * tile
-            row = HALF * half + at
-            f = [fine[half, HALF * k + at : HALF * k + at + 8] for k in range(9)]
-            fiber = [fib[i, row : row + 8] for i in range(3)]
-            inside = (2 <= tile < 6) if half == 0 else tile < 4
-            d, length = tensor_rows(f, fiber, inside)
-            for i in range(6):
-                con[i, row : row + 8] = d[i]
-            if inside:
-                stretch[row : row + 8] = length
-
-        for which, row, outside in ends:
-            corner = cc[1 + half, 11 - 2 * half + which : 12 - 2 * half + which, 0:256]
-            vh[which, outer_p : outer_p + 1] = jnp.where(outside, beside_x[half, 0, row : row + 1], corner)
-        volt = [beside_x[0, 0]] + [pot[x] for x in range(4)] + [beside_x[1, 0]]
-        edge_z = [z_slope(vh[which]) for which in range(2)]
-        for p in range(3 * half, 3 * half + 3):
-            slope_y[p] = from_above(volt[p], vh[1, p : p + 1]) - from_below(volt[p], vh[0, p : p + 1])
-            slope_z[p] = z_slope(volt[p])
-
-        def across(p):
-            return flux(
-                plane(XX, p) + plane(XX, p + 1), volt[p + 1] - volt[p],
-                plane(XY, p) + plane(XY, p + 1), slope_y[p] + slope_y[p + 1],
-                plane(XZ, p) + plane(XZ, p + 1), slope_z[p] + slope_z[p + 1],
+    def halves(sequence):
+        slope_y, slope_z = [None] * 6, [None] * 6
+        for half in sequence:
+            there, _, x = x_sides[half]
+
+            def own_plane(half=half, x=x):
+                beside_x[half, 0] = pot[x]
+                beside_x[half, 1:3] = ang[:, x]
+
+            def own_elements(half=half):
+                cc[1 + half] = cc[0]
+                for which in range(2):
+                    row = 11 - 2 * half + which
+                    cc[1 + half, row : row + 1] = cc[0, 9 + 2 * half + which : 10 + 2 * half + which]
+
+            arrived(there, beside_x.at[half], p_recv.at[half], own_plane)
+            f = fibers(beside_x[half, 1], beside_x[half, 2])
+            outer_p = 5 * half
+            for i in range(3):
+                fib[i, plane_row(outer_p) : plane_row(outer_p) + 16] = f[i]
+            arrived(there, cc.at[1 + half], c_recv.at[half], own_elements)
+
+            onto_lanes(1 + half)
+            t = hat_rows((sub & 1) + 2 * half, 0), hat_rows((sub & 1) + 2 * half, 2 * half - 1)
+            weights = ((0.625, 0.375), (0.375, 0.625), (0.125, 0.875))
+            for k in range(9):
+                side = along_y(1 + half, k)
+                base = HALF * k
+                for number, (a, b) in enumerate(weights[:: 1 - 2 * half]):
+                    for i in range(2):
+                        at = base + 16 * number + 8 * i
+                        crs[half, at : at + 8] = a * side[i] + b * mid[k, i]
+                crs[half, base + 48 : base + 56] = t[0] * mid[k, 2] + t[1] * side[2]
+            c = crs[half]
+            rest = c - c.astype(BF16).astype(F32)
+            left = lax.broadcasted_iota(jnp.int32, c.shape, 1) < 64
+            fine[half] = jnp.dot(
+                jnp.where(left, c, rest).astype(BF16), hat, preferred_element_type=F32
             )
-
-        def within(x):
-            p = x + 1
-            v = volt[p]
-            slope_x = volt[p + 1] - volt[p - 1]
-            d_xy, d_yy, d_yz = plane(XY, p), plane(YY, p), plane(YZ, p)
-            faces = []
-            for which, shift in ((0, from_below), (1, from_above)):
-                row = beside_row(x, which)
-                step = shift(v, vh[which, p : p + 1])
-                step = v - step if which == 0 else step - v
-                faces.append(
-                    flux(
-                        d_yy + shift(d_yy, con[YY, row : row + 1]), step,
-                        d_xy + shift(d_xy, con[XY, row : row + 1]),
-                        slope_x + shift(slope_x, vh[which, p + 1 : p + 2] - vh[which, p - 1 : p]),
-                        d_yz + shift(d_yz, con[YZ, row : row + 1]),
-                        slope_z[p] + shift(slope_z[p], edge_z[which][p : p + 1]),
+            for tile in range(7):
+                at = 8 * tile
+                row = HALF * half + at
+                f = [fine[half, HALF * k + at : HALF * k + at + 8] for k in range(9)]
+                fiber = [fib[i, row : row + 8] for i in range(3)]
+                inside = (2 <= tile < 6) if half == 0 else tile < 4
+                d, length = tensor_rows(f, fiber, inside)
+                for i in range(6):
+                    con[i, row : row + 8] = d[i]
+                if inside:
+                    stretch[row : row + 8] = length
+
+            for which, row, outside in ends:
+                corner = cc[1 + half, 11 - 2 * half + which : 12 - 2 * half + which, 0:256]
+                vh[which, outer_p : outer_p + 1] = jnp.where(outside, beside_x[half, 0, row : row + 1], corner)
+            volt = [beside_x[0, 0]] + [pot[x] for x in range(4)] + [beside_x[1, 0]]
+            edge_z = [z_slope(vh[which]) for which in range(2)]
+            for p in range(3 * half, 3 * half + 3):
+                slope_y[p] = from_above(volt[p], vh[1, p : p + 1]) - from_below(volt[p], vh[0, p : p + 1])
+                slope_z[p] = z_slope(volt[p])
+
+            def across(p):
+                return flux(
+                    plane(XX, p) + plane(XX, p + 1), volt[p + 1] - volt[p],
+                    plane(XY, p) + plane(XY, p + 1), slope_y[p] + slope_y[p + 1],
+                    plane(XZ, p) + plane(XZ, p + 1), slope_z[p] + slope_z[p + 1],
+                )
+
+            def within(x):
+                p = x + 1
+                v = volt[p]
+                slope_x = volt[p + 1] - volt[p - 1]
+                d_xy, d_yy, d_yz = plane(XY, p), plane(YY, p), plane(YZ, p)
+                faces = []
+                for which, shift in ((0, from_below), (1, from_above)):
+                    row = beside_row(x, which)
+                    step = shift(v, vh[which, p : p + 1])
+                    step = v - step if which == 0 else step - v
+                    faces.append(
+                        flux(
+                            d_yy + shift(d_yy, con[YY, row : row + 1]), step,
+                            d_xy + shift(d_xy, con[XY, row : row + 1]),
+                            slope_x + shift(slope_x, vh[which, p + 1 : p + 2] - vh[which, p - 1 : p]),
+                            d_yz + shift(d_yz, con[YZ, row : row + 1]),
+                            slope_z[p] + shift(slope_z[p], edge_z[which][p : p + 1]),
+                        )
                     )
+                faces[0] = jnp.where((row_iota == 0) & first_y, 0.0, faces[0])
+                faces[1] = jnp.where((row_iota == 15) & last_y, 0.0, faces[1])
+                d_xz, d_zz = plane(XZ, p), plane(ZZ, p)
+                upper = flux(
+                    d_zz + onward(d_zz), onward(v) - v,
+                    d_xz + onward(d_xz), slope_x + onward(slope_x),
+                    d_yz + onward(d_yz), slope_y[p] + onward(slope_y[p]),
                 )
-            faces[0] = jnp.where((row_iota == 0) & first_y, 0.0, faces[0])
-            faces[1] = jnp.where((row_iota == 15) & last_y, 0.0, faces[1])
-            d_xz, d_zz = plane(XZ, p), plane(ZZ, p)
-            upper = flux(
-                d_zz + onward(d_zz), onward(v) - v,
-                d_xz + onward(d_xz), slope_x + onward(slope_x),
-                d_yz + onward(d_yz), slope_y[p] + onward(slope_y[p]),
-            )
-            upper = jnp.where(lane == 255, 0.0, upper)
-            w = rec[x]
-            current = excite_gain * v * (v - excite_level) * (v - 1.0) + v * w
-            long = jnp.maximum(stretch[plane_row(p) : plane_row(p) + 16] - 1.0, 0.0)
-            current = current + stretch_gain * long * (v - stretch_reversal)
-            divergent = (faces[1] - faces[0]) + (upper - pltpu.roll(upper, 1, 1))
-            return v + time_step * (divergent - current)
-
-        if half == 0:
-            below = jnp.where(first_x, 0.0, across(0))
-            middle = across(1)
-            onev[0] = within(0) + time_step * (middle - below)
-            onev[1] = within(1) - time_step * middle
-        else:
-            middle = across(2)
-            upper_face = across(3)
-            last_face = jnp.where(last_x, 0.0, across(4))
-            onev[1] = onev[1] + time_step * middle
-            onev[2] = within(2) + time_step * (upper_face - middle)
-            onev[3] = within(3) + time_step * (last_face - upper_face)
+                upper = jnp.where(lane == 255, 0.0, upper)
+                w = rec[x]
+                current = excite_gain * v * (v - excite_level) * (v - 1.0) + v * w
+                long = jnp.maximum(stretch[plane_row(p) : plane_row(p) + 16] - 1.0, 0.0)
+                current = current + stretch_gain * long * (v - stretch_reversal)
+                divergent = (faces[1] - faces[0]) + (upper - pltpu.roll(upper, 1, 1))
+                return v + time_step * (divergent - current)
+
+            if half == 0:
+                face = across(1)
+                onev[0] = within(0) + time_step * (face - jnp.where(first_x, 0.0, across(0)))
+                onev[1] = within(1) - time_step * face
+            else:
+                face = across(3)
+                onev[2] = within(2) + time_step * face
+                onev[3] = within(3) + time_step * (jnp.where(last_x, 0.0, across(4)) - face)
+            if half == sequence[1]:
+                middle = time_step * across(2)
+                onev[1] = onev[1] + middle
+                onev[2] = onev[2] - middle
+
+    upper_first = jnp.logical_or(late, gx == 1)
+
+    @pl.when(upper_first)
+    def _():
+        halves((1, 0))
+
+    @pl.when(jnp.logical_not(upper_first))
+    def _():
+        halves((0, 1))
+
     whole(ag8.at[1:n_y], g_send.at[0]).wait()
     whole(ag1.at[1:n_y], g_send.at[1]).wait()
     for side, (there, _, _) in enumerate(y_sides):
@@ -461,21 +523,14 @@
 
 
 def make_local(n_x, n_y):
-    split = (4, 4) if n_y == 16 else (n_y // 2, 2)
-    outer, inner = split
-
-    def reach(number):
-        o, i = number // inner, number % inner
-        return min(o, outer - o) + 2 * min(i, inner - i)
-
-    order = sorted(range(1, n_y), key=lambda number: -reach(number))
+    assert n_y == 16
 
     def local(potential, recovery, fiber_angles, deform, elem_slot):
         anywhere = pl.BlockSpec(memory_space=pl.ANY)
         cells = (4, 16, 256)
         dma = pltpu.SemaphoreType.DMA
         call = pl.pallas_call(
-            lambda *refs: kernel(n_x, n_y, split, order, *refs),
+            lambda *refs: kernel(n_x, n_y, *refs),
             out_shape=(jax.ShapeDtypeStruct(cells, F32),) * 2,
             in_specs=[pl.BlockSpec(memory_space=pltpu.HBM)] * 5,
             out_specs=(pl.BlockSpec(memory_space=pltpu.VMEM),) * 2,
@@ -503,7 +558,7 @@
                 pltpu.VMEM((2, 8, 256), F32),
                 dma((5,)),
                 dma((2,)),
-                dma((2,)),
+                dma((5, 2)),
                 dma((2,)),
                 dma((2,)),
                 dma((2,)),

time: 22.4 us -> 21.4 us (0.955)
  Pallas kernels: 21.6 us -> 20.6 us
    pallas_call x1, Pallas kernels: 20.9 us -> 19.9 us  [local(): call(*(pltpu.with_memory_space_constraint(a, pltpu.HBM) for a in args))]
where the time goes in v5:
time: 21.4 us; the launch traced here: 21.2 us
  Pallas kernels  20.6 us (96%)
  between operations  0.64 us (3%)
    pallas_call x1, Pallas kernels, local(): call(*(pltpu.with_memory_space_constraint(a, pltpu.HBM) for a in args))  19.9 us
    pallas_call x1, Pallas kernels, local(): pl.pallas_call(store, out_shape=(jax.ShapeDtypeStruct(cells, F32),) * 2,...  0.67 us

profile of v5, /device:TPU:201, one launch (start us, length us, event | category | flops | bytes accessed | tf_op | source)
XLA Modules:
  0.0 21.2 jit_solution(10952651269424620754)
XLA Ops:
  0.6 19.9 %step.1 = (f32[4,16,256]{2,1,0:T(8,128)S(1)}, f32[4,16,256]{2,1,0:T(8,128)S(1)}) custom-call(f32[4,16,256]{2,1,0:T(8,128)} %refs_0_.1, f32[4,16,256]{2,1,0:T(8,128)} %refs_1_.1, f32[2,4,16,256]{3,2,1,0:T(8,128)} %refs_2_.1, f32[9,256]{1,0:T(8,128)} %refs_3_.1, s32[4,64]{1,0:T(4,128)} %bitcast.1), custom_call_target="tpu_custom_call" | custom-call | tf_op jit(solution)/shard_map/step/pallas_call | solution.py:577
  20.5 0.7 %store.1 = (f32[4,16,256]{2,1,0:T(8,128)}, f32[4,16,256]{2,1,0:T(8,128)}) custom-call(f32[4,16,256]{2,1,0:T(8,128)S(1)} %get-tuple-element.4.pot, f32[4,16,256]{2,1,0:T(8,128)S(1)} %get-tuple-element.5.rec), custom_call_target="tpu_custom_call" | custom-call | tf_op jit(solution)/shard_map/store/pallas_call | solution.py:578

commit v6 on v5

--- a/solution.py
+++ b/solution.py
@@ -49,7 +49,7 @@
     return cos_a * cos_e, sin_a * cos_e, sin_e
 
 
-def tensor_rows(f, fiber, want_stretch):
+def tensor_rows(f, fiber, want_stretch, entries):
     def el(i, j):
         return f[3 * (i % 3) + j % 3]
 
@@ -65,12 +65,13 @@
         st = [el(i, 0) * fiber[0] + el(i, 1) * fiber[1] + el(i, 2) * fiber[2] for i in range(3)]
         stretch = jnp.sqrt(st[0] * st[0] + st[1] * st[1] + st[2] * st[2])
     pulled = [cof[0][i] * fiber[0] + cof[1][i] * fiber[1] + cof[2][i] * fiber[2] for i in range(3)]
-    out = []
-    for a, b in ((0, 0), (1, 1), (2, 2), (0, 1), (0, 2), (1, 2)):
+    out = {}
+    cross_scale, fiber_scale = sigma_cross * scale, (sigma_fiber - sigma_cross) * scale
+    scaled = [p * fiber_scale for p in pulled]
+    for number in entries:
+        a, b = ((0, 0), (1, 1), (2, 2), (0, 1), (0, 2), (1, 2))[number]
         metric = cof[0][a] * cof[0][b] + cof[1][a] * cof[1][b] + cof[2][a] * cof[2][b]
-        out.append(
-            (sigma_cross * metric + (sigma_fiber - sigma_cross) * pulled[a] * pulled[b]) * scale
-        )
+        out[number] = cross_scale * metric + scaled[a] * pulled[b]
     return out, stretch
 
 
@@ -89,7 +90,7 @@
 def kernel(
     n_x, n_y,
     pot_in, rec_in, ang_in, def_in, slot_in, onev, onew,
-    pot, rec, ang, slot, dfm, ag8, ag1, ysend, yrecv, srecv, beside_x, cc, s8, s1,
+    pot, rec, ang, slot, dfm, ag8, ag1, ysend, yrecv, srecv, beside_x, cs, cr, s8, s1,
     fib, mid, crs, fine, con, stretch, vh,
     in_sem, g_send, g_recv, s_send, s_recv, h_send, h_recv, p_send, p_recv, c_send, c_recv,
 ):
@@ -214,7 +215,7 @@
                 for i in range(3)
             ]
         )
-        coarse.append(remote(cc.at[0], cc.at[2 - side], c_send.at[side], c_recv.at[1 - side], device))
+        coarse.append(remote(cs.at[side], cr.at[1 - side], c_send.at[side], c_recv.at[1 - side], device))
     for (there, _, _), copy in zip(y_sides, slots):
         send(there, [copy])
 
@@ -234,6 +235,8 @@
     for (there, _, _), copies in zip(x_sides, planes):
         send(there, copies)
 
+    for side in range(2):
+        cs[side, :, 384:512] = jnp.zeros((8, 128), F32)
     for x in range(4):
         v, w = pot[x], rec[x]
         onew[x] = w + time_step * recover_rate * (
@@ -286,11 +289,14 @@
     for at, (o, i) in enumerate(PLACES):
         total = total + jnp.where(source == 4 * o + i, chosen[8 * at : 8 * at + 8], 0.0)
     last = chosen[8 * n_y : 9 * n_y]
-    cc[0, 0:8] = total
-    cc[0, 8:9] = jnp.sum(
+    ninth = jnp.sum(
         jnp.where(place_source == source, last, 0.0),
         axis=0, keepdims=True,
     )
+    for side in range(2):
+        cs[side, :, 0:384] = total
+        for i in range(3):
+            cs[side, i : i + 1, 384:512] = ninth[:, 128 * i : 128 * i + 128]
 
     for side, (there, _, row) in enumerate(y_sides):
 
@@ -299,16 +305,18 @@
 
         arrived(there, yrecv.at[side], h_recv.at[side], own_row)
     for side, (there, _, x) in enumerate(x_sides):
-        row = 9 + 2 * side
         for which in range(2):
-            cc[0, row + which : row + which + 1, 0:256] = yrecv[which, x : x + 1]
+            for i in range(2):
+                row = 3 + 2 * which + i
+                cs[side, row : row + 1, 384:512] = yrecv[which, x : x + 1, 128 * i : 128 * i + 128]
     for (there, _, _), copy in zip(x_sides, coarse):
         send(there, [copy])
 
     def onto_lanes(which):
-        for rows, to in ((slice(0, 8), s8), (slice(8, 9), s1)):
-            for i in range(3):
-                pair = spread(cc[which, rows, 128 * i : 128 * i + 128])
+        held, at = (cr, which - 1) if which else (cs, 0)
+        for i in range(3):
+            pairs = spread(held[at, :, 128 * i : 128 * i + 128]), spread(held[at, i : i + 1, 384:512])
+            for to, pair in zip((s8, s1), pairs):
                 for j in range(2):
                     to[which, :, 128 * (2 * i + j) : 128 * (2 * i + j + 1)] = pair[j]
 
@@ -389,17 +397,14 @@
                 beside_x[half, 1:3] = ang[:, x]
 
             def own_elements(half=half):
-                cc[1 + half] = cc[0]
-                for which in range(2):
-                    row = 11 - 2 * half + which
-                    cc[1 + half, row : row + 1] = cc[0, 9 + 2 * half + which : 10 + 2 * half + which]
+                cr[half] = cs[half]
 
             arrived(there, beside_x.at[half], p_recv.at[half], own_plane)
             f = fibers(beside_x[half, 1], beside_x[half, 2])
             outer_p = 5 * half
             for i in range(3):
                 fib[i, plane_row(outer_p) : plane_row(outer_p) + 16] = f[i]
-            arrived(there, cc.at[1 + half], c_recv.at[half], own_elements)
+            arrived(there, cr.at[half], c_recv.at[half], own_elements)
 
             onto_lanes(1 + half)
             t = hat_rows((sub & 1) + 2 * half, 0), hat_rows((sub & 1) + 2 * half, 2 * half - 1)
@@ -424,14 +429,17 @@
                 f = [fine[half, HALF * k + at : HALF * k + at + 8] for k in range(9)]
                 fiber = [fib[i, row : row + 8] for i in range(3)]
                 inside = (2 <= tile < 6) if half == 0 else tile < 4
-                d, length = tensor_rows(f, fiber, inside)
-                for i in range(6):
+                entries = range(6) if inside else (YY, XY, YZ) if tile == 6 else (XX, XY, XZ)
+                d, length = tensor_rows(f, fiber, inside, entries)
+                for i in entries:
                     con[i, row : row + 8] = d[i]
                 if inside:
                     stretch[row : row + 8] = length
 
             for which, row, outside in ends:
-                corner = cc[1 + half, 11 - 2 * half + which : 12 - 2 * half + which, 0:256]
+                corner = jnp.concatenate(
+                    [cr[half, 3 + 2 * which + i : 4 + 2 * which + i, 384:512] for i in range(2)], axis=1
+                )
                 vh[which, outer_p : outer_p + 1] = jnp.where(outside, beside_x[half, 0, row : row + 1], corner)
             volt = [beside_x[0, 0]] + [pot[x] for x in range(4)] + [beside_x[1, 0]]
             edge_z = [z_slope(vh[which]) for which in range(2)]
@@ -511,7 +519,7 @@
         sent(there, yrecv.at[side], h_send.at[side])
     for side, (there, _, _) in enumerate(x_sides):
         sent(there, beside_x.at[side], p_send.at[side])
-        sent(there, cc.at[1 + side], c_send.at[side])
+        sent(there, cr.at[side], c_send.at[side])
 
 
 def store(pot, rec, pot_out, rec_out, sem):
@@ -546,7 +554,8 @@
                 pltpu.VMEM((2, 16, 256), F32),
                 pltpu.VMEM((2, 4, 64), jnp.int32),
                 pltpu.VMEM((2, 3, 16, 256), F32),
-                pltpu.VMEM((3, 16, 384), F32),
+                pltpu.VMEM((2, 8, 512), F32),
+                pltpu.VMEM((2, 8, 512), F32),
                 pltpu.VMEM((3, 8, 768), F32),
                 pltpu.VMEM((3, 1, 768), F32),
                 pltpu.VMEM((3, ROWS, 256), F32),

time: 21.4 us -> 21.3 us (level)
  no operation moved by 1% of the time
where the time goes in v6:
time: 21.3 us; the launch traced here: 21.1 us
  Pallas kernels  20.5 us (96%)
  between operations  0.64 us (3%)
    pallas_call x1, Pallas kernels, local(): call(*(pltpu.with_memory_space_constraint(a, pltpu.HBM) for a in args))  19.8 us
    pallas_call x1, Pallas kernels, local(): pl.pallas_call(store, out_shape=(jax.ShapeDtypeStruct(cells, F32),) * 2,...  0.67 us

profile of v6, /device:TPU:201, one launch (start us, length us, event | category | flops | bytes accessed | tf_op | source)
XLA Modules:
  0.0 21.1 jit_solution(14853767513721618902)
XLA Ops:
  0.6 19.8 %step.1 = (f32[4,16,256]{2,1,0:T(8,128)S(1)}, f32[4,16,256]{2,1,0:T(8,128)S(1)}) custom-call(f32[4,16,256]{2,1,0:T(8,128)} %refs_0_.1, f32[4,16,256]{2,1,0:T(8,128)} %refs_1_.1, f32[2,4,16,256]{3,2,1,0:T(8,128)} %refs_2_.1, f32[9,256]{1,0:T(8,128)} %refs_3_.1, s32[4,64]{1,0:T(4,128)} %bitcast.1), custom_call_target="tpu_custom_call" | custom-call | tf_op jit(solution)/shard_map/step/pallas_call | solution.py:586
  20.4 0.7 %store.1 = (f32[4,16,256]{2,1,0:T(8,128)}, f32[4,16,256]{2,1,0:T(8,128)}) custom-call(f32[4,16,256]{2,1,0:T(8,128)S(1)} %get-tuple-element.4.pot, f32[4,16,256]{2,1,0:T(8,128)S(1)} %get-tuple-element.5.rec), custom_call_target="tpu_custom_call" | custom-call | tf_op jit(solution)/shard_map/store/pallas_call | solution.py:587

commit v7 on v6

--- a/solution.py
+++ b/solution.py
@@ -404,6 +404,12 @@
             outer_p = 5 * half
             for i in range(3):
                 fib[i, plane_row(outer_p) : plane_row(outer_p) + 16] = f[i]
+            beyond = beside_x[half, 0]
+            inner = (1, 2) if half == 0 else (3, 4)
+            for p in inner:
+                slope_y[p] = from_above(pot[p - 1], vh[1, p : p + 1]) - from_below(pot[p - 1], vh[0, p : p + 1])
+                slope_z[p] = z_slope(pot[p - 1])
+            slope_z[outer_p] = z_slope(beyond)
             arrived(there, cr.at[half], c_recv.at[half], own_elements)
 
             onto_lanes(1 + half)
@@ -443,9 +449,8 @@
                 vh[which, outer_p : outer_p + 1] = jnp.where(outside, beside_x[half, 0, row : row + 1], corner)
             volt = [beside_x[0, 0]] + [pot[x] for x in range(4)] + [beside_x[1, 0]]
             edge_z = [z_slope(vh[which]) for which in range(2)]
-            for p in range(3 * half, 3 * half + 3):
-                slope_y[p] = from_above(volt[p], vh[1, p : p + 1]) - from_below(volt[p], vh[0, p : p + 1])
-                slope_z[p] = z_slope(volt[p])
+            above, below = (vh[which, outer_p : outer_p + 1] for which in (1, 0))
+            slope_y[outer_p] = from_above(beyond, above) - from_below(beyond, below)
 
             def across(p):
                 return flux(

time: 21.3 us -> 21.3 us (level)
  no operation moved by 1% of the time
where the time goes in v7:
time: 21.3 us; the launch traced here: 21.1 us
  Pallas kernels  20.5 us (96%)
  between operations  0.64 us (3%)
    pallas_call x1, Pallas kernels, local(): call(*(pltpu.with_memory_space_constraint(a, pltpu.HBM) for a in args))  19.8 us
    pallas_call x1, Pallas kernels, local(): pl.pallas_call(store, out_shape=(jax.ShapeDtypeStruct(cells, F32),) * 2,...  0.67 us

profile of v7, /device:TPU:201, one launch (start us, length us, event | category | flops | bytes accessed | tf_op | source)
XLA Modules:
  0.0 21.1 jit_solution(12164798653633343761)
XLA Ops:
  0.6 19.8 %step.1 = (f32[4,16,256]{2,1,0:T(8,128)S(1)}, f32[4,16,256]{2,1,0:T(8,128)S(1)}) custom-call(f32[4,16,256]{2,1,0:T(8,128)} %refs_0_.1, f32[4,16,256]{2,1,0:T(8,128)} %refs_1_.1, f32[2,4,16,256]{3,2,1,0:T(8,128)} %refs_2_.1, f32[9,256]{1,0:T(8,128)} %refs_3_.1, s32[4,64]{1,0:T(4,128)} %bitcast.1), custom_call_target="tpu_custom_call" | custom-call | tf_op jit(solution)/shard_map/step/pallas_call | solution.py:591
  20.4 0.7 %store.1 = (f32[4,16,256]{2,1,0:T(8,128)}, f32[4,16,256]{2,1,0:T(8,128)}) custom-call(f32[4,16,256]{2,1,0:T(8,128)S(1)} %get-tuple-element.4.pot, f32[4,16,256]{2,1,0:T(8,128)S(1)} %get-tuple-element.5.rec), custom_call_target="tpu_custom_call" | custom-call | tf_op jit(solution)/shard_map/store/pallas_call | solution.py:592
